TPU v7x, 32 devices: a whole 2x2x4 slice. The times are simulated.
32 devices in a mesh: gx: 8 (over z, y), gy: 2 (over core), gz: 2 (over x).
Axes of the slice: x: 2, y: 2, z: 4, core: 2. Of those that a mesh axis runs over, the one named last changes fastest.
Arguments:
- adjoint_in: float32 [19, 64, 16, 256], P(None, 'gx', 'gy', 'gz'), may hold values from -16 to 16
- forward_states: float32 [2, 19, 64, 16, 256], P(None, None, 'gx', 'gy', 'gz'), may hold values from 0.01 to 0.63
- design: float32 [64, 16, 256], P('gx', 'gy', 'gz'), may hold values from 0 to 1
- solid_mask: int32 [64, 16, 256], P('gx', 'gy', 'gz'), may hold values 0 or 1
- boundary_kind: int32 [64, 16, 256], P('gx', 'gy', 'gz'), may hold values from 0 to 2, as said below
Outputs:
- adjoint_out: float32 [19, 64, 16, 256], P(None, 'gx', 'gy', 'gz')
- sensitivity: float32 [64, 16, 256], P('gx', 'gy', 'gz')
- objective: float32 [], replicated
- sens_rms: float32 [], replicated
Inputs may be any that keep to these rules, and one draw needn't show every extreme that they name: `boundary_kind`: 1 marks inlet cells, 2 outlet cells.
All inputs are finite; a program needn't handle non-finite values. No bound on the sum of `solid_mask` on one device may be relied on, other than what follows from the above.
Results may differ from a plain program's by a relative error of at most 0.0003.
Values sent between devices are 32-bit elements; how exact they have to be, the bound alone decides.
No kernel may reach another device: no remote copies, remote signals or barrier semaphores. Data moves between devices by JAX's collectives and lax.ppermute only.
A program may use at most 64 MiB of HBM per device.

v0:
```python
import jax
import jax.numpy as jnp
import numpy as np
from jax import lax
from jax.sharding import PartitionSpec as P

lattice_table = np.array(
    [
        [0, 0, 0],
        [1, 0, 0],
        [-1, 0, 0],
        [0, 1, 0],
        [0, -1, 0],
        [0, 0, 1],
        [0, 0, -1],
        [1, 1, 0],
        [-1, -1, 0],
        [1, -1, 0],
        [-1, 1, 0],
        [1, 0, 1],
        [-1, 0, -1],
        [1, 0, -1],
        [-1, 0, 1],
        [0, 1, 1],
        [0, -1, -1],
        [0, 1, -1],
        [0, -1, 1],
    ],
    dtype=np.int32,
)
velocity_table = np.array(lattice_table, dtype=np.float32)
lattice_weights = np.array([1.0 / 3] + [1.0 / 18] * 6 + [1.0 / 36] * 12, dtype=np.float32)
opposite_index = [0, 2, 1, 4, 3, 6, 5, 8, 7, 10, 9, 12, 11, 14, 13, 16, 15, 18, 17]
brinkman_max = 4.0
convexity = 0.1
inflow_speed = 0.08


def shifted(block, axis, distance):
    devices = range(lax.axis_size(axis))
    route = [(i - distance, i) for i in devices if i - distance in devices]
    return lax.ppermute(block, axis, route)


def build_relax(lattice):
    cx = lattice[:, 0].astype(np.float32)
    cy = lattice[:, 1].astype(np.float32)
    cz = lattice[:, 2].astype(np.float32)
    csq = cx * cx + cy * cy + cz * cz
    rows = [
        np.ones(19, dtype=np.float32),
        19 * csq - 30,
        (21 * csq * csq - 53 * csq + 24) / 2,
        cx,
        (5 * csq - 9) * cx,
        cy,
        (5 * csq - 9) * cy,
        cz,
        (5 * csq - 9) * cz,
        3 * cx * cx - csq,
        (3 * csq - 5) * (3 * cx * cx - csq),
        cy * cy - cz * cz,
        (3 * csq - 5) * (cy * cy - cz * cz),
        cx * cy,
        cy * cz,
        cx * cz,
        (cy * cy - cz * cz) * cx,
        (cz * cz - cx * cx) * cy,
        (cx * cx - cy * cy) * cz,
    ]
    moments = np.stack(rows).astype(np.float32)
    shear = 1.0 / 0.6
    rates = np.array(
        [
            0,
            1.19,
            1.4,
            0,
            1.2,
            0,
            1.2,
            0,
            1.2,
            shear,
            1.4,
            shear,
            1.4,
            shear,
            shear,
            shear,
            1.98,
            1.98,
            1.98,
        ],
        dtype=np.float32,
    )
    norms = np.sum(moments * moments, axis=1)
    scaled = moments.T * (rates / norms)[None, :]
    return (scaled @ moments).astype(np.float32)


def equilibrium(density, velocity):
    projected = jnp.tensordot(
        velocity_table, velocity, axes=(1, 0), precision=lax.Precision.HIGHEST
    )
    squared = jnp.sum(velocity * velocity, axis=0)
    return (
        lattice_weights[:, None, None, None]
        * density
        * (1.0 + 3.0 * projected + 4.5 * projected * projected - 1.5 * squared)
    )


def post_and_cost(dist, design, solid, kind, weight):
    relax_matrix = build_relax(lattice_table)
    density = jnp.sum(dist, axis=0)
    flux = jnp.tensordot(velocity_table.T, dist, axes=(1, 0), precision=lax.Precision.HIGHEST)
    damping = 1.0 / (1.0 + brinkman_max * convexity * (1.0 - design) / (convexity + design))
    velocity = flux / density * damping
    collided = dist - jnp.tensordot(
        relax_matrix,
        dist - equilibrium(density, velocity),
        axes=(1, 0),
        precision=lax.Precision.HIGHEST,
    )
    ones = jnp.ones_like(density)
    inflow = equilibrium(density, jnp.stack([inflow_speed * ones, 0.0 * ones, 0.0 * ones]))
    outflow = equilibrium(ones, velocity)
    bounced = jnp.stack([dist[k] for k in opposite_index])
    post = jnp.where(
        solid == 1, bounced, jnp.where(kind == 1, inflow, jnp.where(kind == 2, outflow, collided))
    )
    fluid = (solid == 0).astype(jnp.float32)
    cost = weight * fluid * 0.5 * density * jnp.sum(velocity * velocity, axis=0)
    return (post, cost)


def adjoint_step(dist, design, solid, kind, weight, pulled):

    def local(d, g):
        return post_and_cost(d, g, solid, kind, weight)

    outs, backward = jax.vjp(local, dist, design)
    new_adjoint, sens = backward((pulled, jnp.ones_like(outs[1])))
    return (new_adjoint, sens, jnp.sum(outs[1]))


def split_moving(pieces, column):
    upward = [i for i in range(19) if lattice_table[i, column] == 1]
    downward = [i for i in range(19) if lattice_table[i, column] == -1]
    return (
        upward,
        downward,
        jnp.stack([pieces[i] for i in upward]),
        jnp.stack([pieces[i] for i in downward]),
    )


def first_layer(stacked, dim):
    return lax.slice_in_dim(stacked, 0, 1, 1, dim)


def last_layer(stacked, dim):
    length = stacked.shape[dim]
    return lax.slice_in_dim(stacked, length - 1, length, 1, dim)


def place_moving(pieces, upward, downward, up_stack, down_stack, from_above, from_below, dim):
    length = up_stack.shape[dim]
    up_new = jnp.concatenate([lax.slice_in_dim(up_stack, 1, length, 1, dim), from_above], axis=dim)
    down_new = jnp.concatenate(
        [from_below, lax.slice_in_dim(down_stack, 0, length - 1, 1, dim)], axis=dim
    )
    for k, i in enumerate(upward):
        pieces[i] = up_new[k]
    for k, i in enumerate(downward):
        pieces[i] = down_new[k]
    return pieces


def pull_directed(adjoint):
    pieces = [adjoint[i] for i in range(19)]
    upward, downward, up_stack, down_stack = split_moving(pieces, 0)
    from_above = shifted(first_layer(up_stack, 1), "gx", -1)
    from_below = shifted(last_layer(down_stack, 1), "gx", 1)
    pieces = place_moving(pieces, upward, downward, up_stack, down_stack, from_above, from_below, 1)
    upward, downward, up_stack, down_stack = split_moving(pieces, 1)
    from_above = shifted(first_layer(up_stack, 2), "gy", -1)
    from_below = shifted(last_layer(down_stack, 2), "gy", 1)
    pieces = place_moving(pieces, upward, downward, up_stack, down_stack, from_above, from_below, 2)
    upward, downward, up_stack, down_stack = split_moving(pieces, 2)
    from_above = shifted(first_layer(up_stack, 3), "gz", -1)
    from_below = shifted(last_layer(down_stack, 3), "gz", 1)
    pieces = place_moving(pieces, upward, downward, up_stack, down_stack, from_above, from_below, 3)
    return jnp.stack(pieces)


def body(adjoint_in, forward_states, design, solid_mask, boundary_kind):
    block_x, block_y, block_z = design.shape
    whole_x = lax.axis_size("gx") * block_x
    cells = whole_x * lax.axis_size("gy") * block_y * lax.axis_size("gz") * block_z
    xpos = (lax.axis_index("gx") * block_x + jnp.arange(block_x, dtype=jnp.int32)).astype(
        jnp.float32
    )
    weight = (1.0 + 2.0 * xpos / (whole_x - 1))[:, None, None]
    adjoint = adjoint_in
    sens_total = jnp.zeros(design.shape, jnp.float32)
    cost_total = jnp.zeros((), jnp.float32)
    for t in (1, 0):
        pulled = pull_directed(adjoint)
        adjoint, sens_step, cost_step = adjoint_step(
            forward_states[t], design, solid_mask, boundary_kind, weight, pulled
        )
        sens_total = sens_total + sens_step
        cost_total = cost_total + lax.psum(cost_step, ("gx", "gy", "gz"))
    square_total = lax.psum(jnp.sum(sens_total * sens_total), ("gx", "gy", "gz"))
    objective = cost_total / cells
    sens_rms = jnp.sqrt(square_total / cells + 1e-06)
    return (adjoint, sens_total / sens_rms, objective, sens_rms)


def solution(mesh):
    placed = (
        P(None, "gx", "gy", "gz"),
        P(None, None, "gx", "gy", "gz"),
        P("gx", "gy", "gz"),
        P("gx", "gy", "gz"),
        P("gx", "gy", "gz"),
    )
    return jax.shard_map(
        body,
        mesh=mesh,
        in_specs=placed,
        out_specs=(P(None, "gx", "gy", "gz"), P("gx", "gy", "gz"), P(), P()),
        check_vma=False,
    )
```

profile of v0, /device:TPU:0, one launch (start us, length us, event | category | flops | bytes accessed | tf_op | source)
XLA Modules:
  0.0 134.2 jit_solution(16861905017159966916)
XLA Ops:
  0.6 1.8 %fusion.116 = (f32[1,8,8,128]{3,2,1,0:T(8,128)S(1)}, f32[1,8,8,128]{3,2,1,0:T(8,128)}, f32[1,8,8,128]{3,2,1,0:T(8,128)}, f32[1,8,8,128]{3,2,1,0:T(8,128)}, f32[1...) fusion(f32[19,8,8,128]{3,2,1,0:T(8,128)} %param.21), kind=kLoop, calls=%fused_computation.221 | loop fusion | bytes 1245184 | tf_op jit(solution)/shard_map/slice | solution.py:182
  3.3 5.5 %collective-permute-start.1 = (f32[5,1,8,128]{3,0,2,1:T(8,128)}, f32[5,1,8,128]{3,0,2,1:T(8,128)}, u32[]{:S(2)}, u32[]{:S(2)}) collective-permute-start(f32[5,1,8,128]{3,0,2,1:T(8,128)} %slice.484), channel_id=1, source_target_pairs={{0,4},{4,8},{8,12},{12,16},{16,20},{20,24},{24,28},{1,5},{5,9},{9,... | collective-permute-start | bytes 61448 | tf_op jit(solution)/shard_map/ppermute | solution.py:42
  17.8 1.5 %collective-permute-start.3 = (f32[5,8,1,128]{3,0,2,1:T(8,128)S(1)}, f32[5,8,1,128]{3,0,2,1:T(8,128)S(1)}, u32[]{:S(2)}, u32[]{:S(2)}) collective-permute-start(f32[5,8,1,128]{3,0,2,1:T(8,128)S(1)} %slice.488), channel_id=1, source_target_pairs={{0,2},{1,3},{4,6},{5,7},{8,10},{9,11},{12,14},{13,15},{16,18},{17,... | collective-permute-start | bytes 61448 | tf_op jit(solution)/shard_map/ppermute | solution.py:42
  19.6 1.3 collective-permute-start.2
  21.0 1.7 %collective-permute-done.2 = f32[5,8,1,128]{3,0,2,1:T(8,128)S(1)} collective-permute-done((f32[5,8,1,128]{3,0,2,1:T(8,128)S(1)}, f32[5,8,1,128]{3,0,2,1:T(8,128)S(1)}, u32[]{:S(2)}, u32[]{:S(2)}) %collective-permute-start.2) | collective-permute-done | bytes 20512 | tf_op jit(solution)/shard_map/ppermute | solution.py:42
  23.2 3.4 %collective-permute-start.5 = (f32[5,8,8,1]{3,0,2,1:T(8,128)S(1)}, f32[5,8,8,1]{3,0,2,1:T(8,128)S(1)}, u32[]{:S(2)}, u32[]{:S(2)}) collective-permute-start(f32[5,8,8,1]{3,0,2,1:T(8,128)S(1)} %slice.492), channel_id=1, source_target_pairs={{0,1},{2,3},{4,5},{6,7},{8,9},{10,11},{12,13},{14,15},{16,17},{18,... | collective-permute-start | bytes 3848 | tf_op jit(solution)/shard_map/ppermute | solution.py:42
  27.1 1.5 %collective-permute-start.4 = (f32[5,8,8,1]{3,0,2,1:T(8,128)S(1)}, f32[5,8,8,1]{3,0,2,1:T(8,128)S(1)}, u32[]{:S(2)}, u32[]{:S(2)}) collective-permute-start(f32[5,8,8,1]{3,0,2,1:T(8,128)S(1)} %bitcast.56), channel_id=1, source_target_pairs={{1,0},{3,2},{5,4},{7,6},{9,8},{11,10},{13,12},{15,14},{17,16},{19,... | collective-permute-start | bytes 3848 | tf_op jit(solution)/shard_map/ppermute | solution.py:42
  28.6 3.9 %collective-permute-done.5 = f32[5,8,8,1]{3,0,2,1:T(8,128)S(1)} collective-permute-done((f32[5,8,8,1]{3,0,2,1:T(8,128)S(1)}, f32[5,8,8,1]{3,0,2,1:T(8,128)S(1)}, u32[]{:S(2)}, u32[]{:S(2)}) %collective-permute-start.5) | collective-permute-done | bytes 1312 | tf_op jit(solution)/shard_map/ppermute | solution.py:42
  32.9 4.2 %collective-permute-done.4 = f32[5,8,8,1]{3,0,2,1:T(8,128)S(1)} collective-permute-done((f32[5,8,8,1]{3,0,2,1:T(8,128)S(1)}, f32[5,8,8,1]{3,0,2,1:T(8,128)S(1)}, u32[]{:S(2)}, u32[]{:S(2)}) %collective-permute-start.4) | collective-permute-done | bytes 1312 | tf_op jit(solution)/shard_map/ppermute | solution.py:42
  38.3 2.8 %multiply_reduce_fusion.1 = (f32[8,8,128]{2,1,0:T(8,128)S(1)}, f32[8,8,128]{2,1,0:T(8,128)S(1)}, f32[8,8,128]{2,1,0:T(8,128)S(1)}, f32[8,8,128]{2,1,0:T(8,128)S(...) fusion(f32[19,8,8,128]{3,0,2,1:T(8,128)} %constant.157, f32[19,8,8,128]{3,0,2,1:T(8,128)S(1)} %stack.50, ...), kind=kOutput, calls=%fused_computation.51 | convolution fusion | flops 39657472 | bytes 3335664 | tf_op jit(solution)/shard_map/transpose(jvp())/dot_general | solution.py:120
  43.6 1.3 multiply_reduce_fusion.8
  44.9 2.2 %fusion.1 = f32[19,8,8,128]{3,0,2,1:T(8,128)S(1)} fusion(f32[3,19,1,1]{1,0,3,2:T(4,128)S(1)} %copy-done.18, f32[19,8,8,128]{3,0,2,1:T(8,128)S(1)} %get-tuple-element.169, f32[1,8,8,128]{3,0,2,1:T(1,128)S(1)} %get-tuple-element.78, f32[1,8,8,128]{3,0,2,1:T(1,128)S(1)} %get-tuple-element.79, f32[1,8,8,128]{3,0,2,1:T(1,128)S(1)} %get-tuple-element.80, ...), kind=kOutput, calls=%fused_computation.3 | convolution fusion | flops 9854976 | bytes 2679031 | tf_op jit(solution)/shard_map/transpose(jvp())/dot_general | solution.py:117
  48.0 4.4 %collective-permute-start.7 = (f32[5,1,8,128]{3,0,2,1:T(8,128)S(1)}, f32[5,1,8,128]{3,0,2,1:T(8,128)S(1)}, u32[]{:S(2)}, u32[]{:S(2)}) collective-permute-start(f32[5,1,8,128]{3,0,2,1:T(8,128)S(1)} %slice.507), channel_id=1, source_target_pairs={{0,4},{4,8},{8,12},{12,16},{16,20},{20,24},{24,28},{1,5},{5,9},{9,... | collective-permute-start | bytes 61448 | tf_op jit(solution)/shard_map/ppermute | solution.py:42
  52.7 1.3 collective-permute-start.6
  54.1 4.4 %collective-permute-done.6 = f32[5,1,8,128]{3,0,2,1:T(8,128)S(1)} collective-permute-done((f32[5,1,8,128]{3,0,2,1:T(8,128)S(1)}, f32[5,1,8,128]{3,0,2,1:T(8,128)S(1)}, u32[]{:S(2)}, u32[]{:S(2)}) %collective-permute-start.6) | collective-permute-done | bytes 20512 | tf_op jit(solution)/shard_map/ppermute | solution.py:42
  64.1 1.7 %collective-permute-done.8 = f32[5,8,1,128]{3,0,2,1:T(8,128)S(1)} collective-permute-done((f32[5,8,1,128]{3,0,2,1:T(8,128)S(1)}, f32[5,8,1,128]{3,0,2,1:T(8,128)S(1)}, u32[]{:S(2)}, u32[]{:S(2)}) %collective-permute-start.8) | collective-permute-done | bytes 20512 | tf_op jit(solution)/shard_map/ppermute | solution.py:42
  66.3 1.5 %collective-permute-start.11 = (f32[5,8,8,1]{3,0,2,1:T(8,128)S(1)}, f32[5,8,8,1]{3,0,2,1:T(8,128)S(1)}, u32[]{:S(2)}, u32[]{:S(2)}) collective-permute-start(f32[5,8,8,1]{3,0,2,1:T(8,128)S(1)} %slice.523), channel_id=1, source_target_pairs={{0,1},{2,3},{4,5},{6,7},{8,9},{10,11},{12,13},{14,15},{16,17},{18,... | collective-permute-start | bytes 3848 | tf_op jit(solution)/shard_map/ppermute | solution.py:42
  68.2 1.5 %collective-permute-start.10 = (f32[5,8,8,1]{3,0,2,1:T(8,128)S(1)}, f32[5,8,8,1]{3,0,2,1:T(8,128)S(1)}, u32[]{:S(2)}, u32[]{:S(2)}) collective-permute-start(f32[5,8,8,1]{3,0,2,1:T(8,128)S(1)} %bitcast.57), channel_id=1, source_target_pairs={{1,0},{3,2},{5,4},{7,6},{9,8},{11,10},{13,12},{15,14},{17,16},{19,... | collective-permute-start | bytes 3848 | tf_op jit(solution)/shard_map/ppermute | solution.py:42
  69.7 4.0 %collective-permute-done.11 = f32[5,8,8,1]{3,0,2,1:T(8,128)S(1)} collective-permute-done((f32[5,8,8,1]{3,0,2,1:T(8,128)S(1)}, f32[5,8,8,1]{3,0,2,1:T(8,128)S(1)}, u32[]{:S(2)}, u32[]{:S(2)}) %collective-permute-start.11) | collective-permute-done | bytes 1312 | tf_op jit(solution)/shard_map/ppermute | solution.py:42
  74.1 4.2 %collective-permute-done.10 = f32[5,8,8,1]{3,0,2,1:T(8,128)S(1)} collective-permute-done((f32[5,8,8,1]{3,0,2,1:T(8,128)S(1)}, f32[5,8,8,1]{3,0,2,1:T(8,128)S(1)}, u32[]{:S(2)}, u32[]{:S(2)}) %collective-permute-start.10) | collective-permute-done | bytes 1312 | tf_op jit(solution)/shard_map/ppermute | solution.py:42
  79.5 2.8 %multiply_reduce_fusion = (f32[8,8,128]{2,1,0:T(8,128)S(1)}, f32[8,8,128]{2,1,0:T(8,128)S(1)}, f32[8,8,128]{2,1,0:T(8,128)S(1)}, f32[8,8,128]{2,1,0:T(8,128)S(1)...) fusion(f32[19,8,8,128]{3,0,2,1:T(8,128)} %constant.157, f32[19,8,8,128]{3,0,2,1:T(8,128)S(1)} %stack.57, ...), kind=kOutput, calls=%fused_computation.40 | convolution fusion | flops 39657472 | bytes 3335664 | tf_op jit(solution)/shard_map/transpose(jvp())/dot_general | solution.py:120
  83.3 1.6 %multiply_reduce_fusion.2 = (f32[8,8,128]{2,1,0:T(8,128)S(1)}, f32[8,8,128]{2,1,0:T(8,128)S(1)}, f32[3,8,8,128]{3,0,2,1:T(4,128)}) fusion(f32[3,8,8,128]{3,0,2,1:T(4,128)S(1)} %fusion.28, f32[8,8,128]{2,1,0:T(8,128)S(1)} %get-tuple-element.8, f32[8,8,128]{2,1,0:T(8,128)S(1)} %get-tuple-element.160, f32[8,8,128]{2,1,0:T(8,128)S(1)} %fusion.98, ...), kind=kOutput, calls=%fused_computation.106 | convolution fusion | flops 7340032 | bytes 1704240 | tf_op jit(solution)/shard_map/transpose(jvp())/dot_general | solution.py:103
  85.6 40.5 %all-reduce.36 = (f32[]{:T(128)}, f32[]{:T(128)}) all-reduce(f32[]{:T(128)} %get-tuple-element.34, f32[]{:T(128)S(6)} %add.153), channel_id=1, replica_groups=mesh['gx'=8,'gy'=2,'gz'=2] {'gx','gy','gz'}, use_global_device_ids=true, to_apply=%region_17.18 | all-reduce | flops 2 | bytes 16 | tf_op jit(solution)/shard_map/psum | solution.py:216
  128.1 2.2 %fusion = f32[19,8,8,128]{3,0,2,1:T(8,128)S(1)} fusion(f32[3,19,1,1]{1,0,3,2:T(4,128)S(1)} %copy-done.19, f32[19,8,8,128]{3,0,2,1:T(8,128)S(1)} %copy-done.27, f32[1,8,8,128]{3,0,2,1:T(1,128)S(1)} %get-tuple-element.41, f32[1,8,8,128]{3,0,2,1:T(1,128)S(1)} %get-tuple-element.42, f32[1,8,8,128]{3,0,2,1:T(1,128)S(1)} %get-tuple-element.43, ...), kind=kOutput, calls=%fused_computation.1 | convolution fusion | flops 9854976 | bytes 2679031 | tf_op jit(solution)/shard_map/transpose(jvp())/dot_general | solution.py:117
  (141 shorter events, 26.4 us)
Async XLA Ops:
  0.6 10.3 %copy-start = (f32[2,19,8,8,128]{4,3,2,1,0:T(8,128)S(1)}, f32[2,19,8,8,128]{4,3,2,1,0:T(8,128)}, u32[]{:S(2)}) copy-start(f32[2,19,8,8,128]{4,3,2,1,0:T(8,128)} %param.22) | copy-start | bytes 3735556
  3.3 12.0 %collective-permute-start.1 = (f32[5,1,8,128]{3,0,2,1:T(8,128)}, f32[5,1,8,128]{3,0,2,1:T(8,128)}, u32[]{:S(2)}, u32[]{:S(2)}) collective-permute-start(f32[5,1,8,128]{3,0,2,1:T(8,128)} %slice.484), channel_id=1, source_target_pairs={{0,4},{4,8},{8,12},{12,16},{16,20},{20,24},{24,28},{1,5},{5,9},{9,... | collective-permute-start | bytes 61448 | tf_op jit(solution)/shard_map/ppermute | solution.py:42
  9.6 6.7 %collective-permute-start = (f32[5,1,8,128]{3,0,2,1:T(8,128)}, f32[5,1,8,128]{3,0,2,1:T(8,128)}, u32[]{:S(2)}, u32[]{:S(2)}) collective-permute-start(f32[5,1,8,128]{3,0,2,1:T(8,128)} %slice.483), channel_id=1, source_target_pairs={{4,0},{8,4},{12,8},{16,12},{20,16},{24,20},{28,24},{5,1},{9,5},{13... | collective-permute-start | bytes 61448 | tf_op jit(solution)/shard_map/ppermute | solution.py:42
  15.2 67.2 %copy-start.13 = (pred[8,8,128]{2,1,0:T(8,128)(4,1)}, pred[8,8,128]{2,1,0:T(8,128)(4,1)S(1)}, u32[]{:S(2)}) copy-start(pred[8,8,128]{2,1,0:T(8,128)(4,1)S(1)} %get-tuple-element.164) | copy-start | bytes 24580
  15.2 67.2 %copy-start.15 = (pred[8,8,128]{2,1,0:T(8,128)(4,1)}, pred[8,8,128]{2,1,0:T(8,128)(4,1)S(1)}, u32[]{:S(2)}) copy-start(pred[8,8,128]{2,1,0:T(8,128)(4,1)S(1)} %get-tuple-element.165) | copy-start | bytes 24580
  17.8 3.1 %collective-permute-start.3 = (f32[5,8,1,128]{3,0,2,1:T(8,128)S(1)}, f32[5,8,1,128]{3,0,2,1:T(8,128)S(1)}, u32[]{:S(2)}, u32[]{:S(2)}) collective-permute-start(f32[5,8,1,128]{3,0,2,1:T(8,128)S(1)} %slice.488), channel_id=1, source_target_pairs={{0,2},{1,3},{4,6},{5,7},{8,10},{9,11},{12,14},{13,15},{16,18},{17,... | collective-permute-start | bytes 61448 | tf_op jit(solution)/shard_map/ppermute | solution.py:42
  19.6 3.1 %collective-permute-start.2 = (f32[5,8,1,128]{3,0,2,1:T(8,128)S(1)}, f32[5,8,1,128]{3,0,2,1:T(8,128)S(1)}, u32[]{:S(2)}, u32[]{:S(2)}) collective-permute-start(f32[5,8,1,128]{3,0,2,1:T(8,128)S(1)} %slice.487), channel_id=1, source_target_pairs={{2,0},{3,1},{6,4},{7,5},{10,8},{11,9},{14,12},{15,13},{18,16},{19,... | collective-permute-start | bytes 61448 | tf_op jit(solution)/shard_map/ppermute | solution.py:42
  23.2 9.3 %collective-permute-start.5 = (f32[5,8,8,1]{3,0,2,1:T(8,128)S(1)}, f32[5,8,8,1]{3,0,2,1:T(8,128)S(1)}, u32[]{:S(2)}, u32[]{:S(2)}) collective-permute-start(f32[5,8,8,1]{3,0,2,1:T(8,128)S(1)} %slice.492), channel_id=1, source_target_pairs={{0,1},{2,3},{4,5},{6,7},{8,9},{10,11},{12,13},{14,15},{16,17},{18,... | collective-permute-start | bytes 3848 | tf_op jit(solution)/shard_map/ppermute | solution.py:42
  27.1 10.0 %collective-permute-start.4 = (f32[5,8,8,1]{3,0,2,1:T(8,128)S(1)}, f32[5,8,8,1]{3,0,2,1:T(8,128)S(1)}, u32[]{:S(2)}, u32[]{:S(2)}) collective-permute-start(f32[5,8,8,1]{3,0,2,1:T(8,128)S(1)} %bitcast.56), channel_id=1, source_target_pairs={{1,0},{3,2},{5,4},{7,6},{9,8},{11,10},{13,12},{15,14},{17,16},{19,... | collective-permute-start | bytes 3848 | tf_op jit(solution)/shard_map/ppermute | solution.py:42
  32.9 5.4 %copy-start.20 = (f32[19,19,1,1]{0,1,3,2:T(8,128)S(1)}, f32[19,19,1,1]{0,1,3,2:T(8,128)}, u32[]{:S(2)}) copy-start(f32[19,19,1,1]{0,1,3,2:T(8,128)} %constant.158) | copy-start | bytes 4336
  48.0 6.0 %collective-permute-start.7 = (f32[5,1,8,128]{3,0,2,1:T(8,128)S(1)}, f32[5,1,8,128]{3,0,2,1:T(8,128)S(1)}, u32[]{:S(2)}, u32[]{:S(2)}) collective-permute-start(f32[5,1,8,128]{3,0,2,1:T(8,128)S(1)} %slice.507), channel_id=1, source_target_pairs={{0,4},{4,8},{8,12},{12,16},{16,20},{20,24},{24,28},{1,5},{5,9},{9,... | collective-permute-start | bytes 61448 | tf_op jit(solution)/shard_map/ppermute | solution.py:42
  52.7 5.8 %collective-permute-start.6 = (f32[5,1,8,128]{3,0,2,1:T(8,128)S(1)}, f32[5,1,8,128]{3,0,2,1:T(8,128)S(1)}, u32[]{:S(2)}, u32[]{:S(2)}) collective-permute-start(f32[5,1,8,128]{3,0,2,1:T(8,128)S(1)} %slice.501), channel_id=1, source_target_pairs={{4,0},{8,4},{12,8},{16,12},{20,16},{24,20},{28,24},{5,1},{9,5},{13... | collective-permute-start | bytes 61448 | tf_op jit(solution)/shard_map/ppermute | solution.py:42
  58.9 5.1 %collective-permute-start.9 = (f32[5,8,1,128]{3,0,2,1:T(8,128)S(1)}, f32[5,8,1,128]{3,0,2,1:T(8,128)S(1)}, u32[]{:S(2)}, u32[]{:S(2)}) collective-permute-start(f32[5,8,1,128]{3,0,2,1:T(8,128)S(1)} %slice.517), channel_id=1, source_target_pairs={{0,2},{1,3},{4,6},{5,7},{8,10},{9,11},{12,14},{13,15},{16,18},{17,... | collective-permute-start | bytes 61448 | tf_op jit(solution)/shard_map/ppermute | solution.py:42
  62.7 3.1 %collective-permute-start.8 = (f32[5,8,1,128]{3,0,2,1:T(8,128)S(1)}, f32[5,8,1,128]{3,0,2,1:T(8,128)S(1)}, u32[]{:S(2)}, u32[]{:S(2)}) collective-permute-start(f32[5,8,1,128]{3,0,2,1:T(8,128)S(1)} %slice.513), channel_id=1, source_target_pairs={{2,0},{3,1},{6,4},{7,5},{10,8},{11,9},{14,12},{15,13},{18,16},{19,... | collective-permute-start | bytes 61448 | tf_op jit(solution)/shard_map/ppermute | solution.py:42
  66.3 7.5 %collective-permute-start.11 = (f32[5,8,8,1]{3,0,2,1:T(8,128)S(1)}, f32[5,8,8,1]{3,0,2,1:T(8,128)S(1)}, u32[]{:S(2)}, u32[]{:S(2)}) collective-permute-start(f32[5,8,8,1]{3,0,2,1:T(8,128)S(1)} %slice.523), channel_id=1, source_target_pairs={{0,1},{2,3},{4,5},{6,7},{8,9},{10,11},{12,13},{14,15},{16,17},{18,... | collective-permute-start | bytes 3848 | tf_op jit(solution)/shard_map/ppermute | solution.py:42
  68.2 10.1 %collective-permute-start.10 = (f32[5,8,8,1]{3,0,2,1:T(8,128)S(1)}, f32[5,8,8,1]{3,0,2,1:T(8,128)S(1)}, u32[]{:S(2)}, u32[]{:S(2)}) collective-permute-start(f32[5,8,8,1]{3,0,2,1:T(8,128)S(1)} %bitcast.57), channel_id=1, source_target_pairs={{1,0},{3,2},{5,4},{7,6},{9,8},{11,10},{13,12},{15,14},{17,16},{19,... | collective-permute-start | bytes 3848 | tf_op jit(solution)/shard_map/ppermute | solution.py:42
  74.1 5.4 %copy-start.11 = (f32[8,8,128]{2,1,0:T(8,128)S(1)}, f32[8,8,128]{2,1,0:T(8,128)}, u32[]{:S(2)}) copy-start(f32[8,8,128]{2,1,0:T(8,128)} %get-tuple-element.161) | copy-start | bytes 98308
  74.1 5.4 %copy-start.21 = (f32[19,19,1,1]{0,1,3,2:T(8,128)S(1)}, f32[19,19,1,1]{0,1,3,2:T(8,128)}, u32[]{:S(2)}) copy-start(f32[19,19,1,1]{0,1,3,2:T(8,128)} %constant.158) | copy-start | bytes 4336
  84.9 43.1 %copy-start.14 = (pred[8,8,128]{2,1,0:T(8,128)(4,1)S(1)}, pred[8,8,128]{2,1,0:T(8,128)(4,1)}, u32[]{:S(2)}) copy-start(pred[8,8,128]{2,1,0:T(8,128)(4,1)} %copy-done.13) | copy-start | bytes 24580
  84.9 43.1 %copy-start.16 = (pred[8,8,128]{2,1,0:T(8,128)(4,1)S(1)}, pred[8,8,128]{2,1,0:T(8,128)(4,1)}, u32[]{:S(2)}) copy-start(pred[8,8,128]{2,1,0:T(8,128)(4,1)} %copy-done.15) | copy-start | bytes 24580
  85.0 43.1 %copy-start.19 = (f32[3,19,1,1]{1,0,3,2:T(4,128)S(1)}, f32[3,19,1,1]{1,0,3,2:T(4,128)}, u32[]{:S(2)}) copy-start(f32[3,19,1,1]{1,0,3,2:T(4,128)} %constant.159) | copy-start | bytes 688
  85.0 43.1 %copy-start.23 = (pred[19]{0:T(512)(128)(4,1)S(1)}, pred[19]{0:T(512)(128)(4,1)}, u32[]{:S(2)}) copy-start(pred[19]{0:T(512)(128)(4,1)} %constant.56.clone.1) | copy-start | bytes 61
  85.0 43.1 %copy-start.27 = (f32[19,8,8,128]{3,0,2,1:T(8,128)S(1)}, f32[19,8,8,128]{3,0,2,1:T(8,128)}, u32[]{:S(2)}) copy-start(f32[19,8,8,128]{3,0,2,1:T(8,128)} %copy-done.26) | copy-start | bytes 1867780
  85.0 43.1 %copy-start.28 = (f32[3,8,8,128]{3,0,2,1:T(4,128)S(1)}, f32[3,8,8,128]{3,0,2,1:T(4,128)}, u32[]{:S(2)}) copy-start(f32[3,8,8,128]{3,0,2,1:T(4,128)} %get-tuple-element.172) | copy-start | bytes 294916
  (17 other events, 48.7 us)
where the time goes:
time: 135 us; the launch traced here: 134 us
  blocking collectives  40.5 us (30%)
  starting transfers between devices  25.6 us (19%)
  waiting for transfers between devices  24.1 us (18%)
  matrix products  18 us (13%)
  local copies, waits for them, and re-layouts  11.4 us (8%)
  other arithmetic  7.97 us (6%)
  between operations  6.56 us (5%)
    psum x1, blocking collectives, body(): lax.psum(jnp.sum(sens_total * sens_total), ('gx', 'gy', 'gz'))  40.5 us
    ppermute x12, starting transfers between devices, shifted(): return lax.ppermute(block, axis, route)  25.6 us
    ppermute x12, waiting for transfers between devices, shifted(): return lax.ppermute(block, axis, route)  24.1 us
    dot_general x6, matrix products, equilibrium(): jnp.tensordot(velocity_table, velocity, axes=(1, 0), precision=lax.Precis...  6.21 us
    dot_general x4, matrix products, post_and_cost(): jnp.tensordot(velocity_table.T, dist, axes=(1, 0), precision=lax.Precisio...  6.2 us
    dot_general x2, matrix products, post_and_cost(): jnp.tensordot(relax_matrix, dist - equilibrium(density, velocity), axes=(...  5.63 us
  transfers between devices with their start and end apart: 12, of which 7 were waited for; matrix products, arithmetic and copies ran while one was open for 7% of the time, Pallas kernels for 0%

commit v1 on v0

--- a/solution.py
+++ b/solution.py
@@ -195,6 +195,15 @@
     return jnp.stack(pieces)
 
 
+def sum_everywhere(cost, square):
+    axes = ("gx", "gy", "gz")
+    devices = lax.axis_size(axes)
+    lane = lax.broadcasted_iota(jnp.int32, (devices, 1, 128), 2)
+    sent = jnp.where(lane < 64, cost, square)
+    got = jnp.sum(lax.all_to_all(sent, axes, 0, 0), axis=0)
+    return got[0, 0], got[0, 64]
+
+
 def body(adjoint_in, forward_states, design, solid_mask, boundary_kind):
     block_x, block_y, block_z = design.shape
     whole_x = lax.axis_size("gx") * block_x
@@ -212,8 +221,9 @@
             forward_states[t], design, solid_mask, boundary_kind, weight, pulled
         )
         sens_total = sens_total + sens_step
-        cost_total = cost_total + lax.psum(cost_step, ("gx", "gy", "gz"))
-    square_total = lax.psum(jnp.sum(sens_total * sens_total), ("gx", "gy", "gz"))
+        cost_total = cost_total + cost_step
+    square_total = jnp.sum(sens_total * sens_total)
+    cost_total, square_total = sum_everywhere(cost_total, square_total)
     objective = cost_total / cells
     sens_rms = jnp.sqrt(square_total / cells + 1e-06)
     return (adjoint, sens_total / sens_rms, objective, sens_rms)

time: 135 us -> 105 us (0.78)
  blocking collectives: 40.5 us -> 0 us
  starting transfers between devices: 25.6 us -> 30.8 us
  waiting for transfers between devices: 24.1 us -> 27.4 us
    psum x1 -> x0, blocking collectives: 40.5 us -> none  [body(): lax.psum(jnp.sum(sens_total * sens_total), ('gx', 'gy', 'gz'))]
    all_to_all x0 -> x1, starting transfers between devices: none -> 5.13 us  [sum_everywhere(): got = jnp.sum(lax.all_to_all(sent, axes, 0, 0), axis=0)]
    all_to_all x0 -> x1, waiting for transfers between devices: none -> 3.28 us  [sum_everywhere(): got = jnp.sum(lax.all_to_all(sent, axes, 0, 0), axis=0)]
  transfers between devices with their start and end apart: 12 -> 13, of which waited for: 7 -> 8; matrix products, arithmetic and copies ran while one was open for 7% -> 12% of each run, Pallas kernels for 0% -> 0%
where the time goes in v1:
time: 105 us; the launch traced here: 104 us
  starting transfers between devices  30.8 us (29%)
  waiting for transfers between devices  27.4 us (26%)
  matrix products  18 us (17%)
  local copies, waits for them, and re-layouts  12.6 us (12%)
  other arithmetic  8.57 us (8%)
  between operations  6.58 us (6%)
    ppermute x12, starting transfers between devices, shifted(): return lax.ppermute(block, axis, route)  25.6 us
    ppermute x12, waiting for transfers between devices, shifted(): return lax.ppermute(block, axis, route)  24.1 us
    dot_general x6, matrix products, equilibrium(): jnp.tensordot(velocity_table, velocity, axes=(1, 0), precision=lax.Precis...  6.21 us
    dot_general x4, matrix products, post_and_cost(): jnp.tensordot(velocity_table.T, dist, axes=(1, 0), precision=lax.Precisio...  6.2 us
    dot_general x2, matrix products, post_and_cost(): jnp.tensordot(relax_matrix, dist - equilibrium(density, velocity), axes=(...  5.63 us
    all_to_all x1, starting transfers between devices, sum_everywhere(): got = jnp.sum(lax.all_to_all(sent, axes, 0, 0), axis=0)  5.13 us
    all_to_all x1, waiting for transfers between devices, sum_everywhere(): got = jnp.sum(lax.all_to_all(sent, axes, 0, 0), axis=0)  3.28 us
    slice x2, local copies, waits for them, and re-layouts, pull_directed(): pieces = [adjoint[i] for i in range(19)]  2.37 us
  transfers between devices with their start and end apart: 13, of which 8 were waited for; matrix products, arithmetic and copies ran while one was open for 12% of the time, Pallas kernels for 0%

profile of v1, /device:TPU:0, one launch (start us, length us, event | category | flops | bytes accessed | tf_op | source)
XLA Modules:
  0.0 103.9 jit_solution(16494013791427874648)
XLA Ops:
  0.6 1.8 %fusion.116 = (f32[1,8,8,128]{3,2,1,0:T(8,128)S(1)}, f32[1,8,8,128]{3,2,1,0:T(8,128)}, f32[1,8,8,128]{3,2,1,0:T(8,128)}, f32[1,8,8,128]{3,2,1,0:T(8,128)}, f32[1...) fusion(f32[19,8,8,128]{3,2,1,0:T(8,128)} %param.21), kind=kLoop, calls=%fused_computation.222 | loop fusion | bytes 1245184 | tf_op jit(solution)/shard_map/slice | solution.py:182
  3.3 5.5 %collective-permute-start.1 = (f32[5,1,8,128]{3,0,2,1:T(8,128)}, f32[5,1,8,128]{3,0,2,1:T(8,128)}, u32[]{:S(2)}, u32[]{:S(2)}) collective-permute-start(f32[5,1,8,128]{3,0,2,1:T(8,128)} %slice.492), channel_id=1, source_target_pairs={{0,4},{4,8},{8,12},{12,16},{16,20},{20,24},{24,28},{1,5},{5,9},{9,... | collective-permute-start | bytes 61448 | tf_op jit(solution)/shard_map/ppermute | solution.py:42
  17.7 1.5 %collective-permute-start.3 = (f32[5,8,1,128]{3,0,2,1:T(8,128)S(1)}, f32[5,8,1,128]{3,0,2,1:T(8,128)S(1)}, u32[]{:S(2)}, u32[]{:S(2)}) collective-permute-start(f32[5,8,1,128]{3,0,2,1:T(8,128)S(1)} %slice.496), channel_id=1, source_target_pairs={{0,2},{1,3},{4,6},{5,7},{8,10},{9,11},{12,14},{13,15},{16,18},{17,... | collective-permute-start | bytes 61448 | tf_op jit(solution)/shard_map/ppermute | solution.py:42
  19.6 1.3 %collective-permute-start.2 = (f32[5,8,1,128]{3,0,2,1:T(8,128)S(1)}, f32[5,8,1,128]{3,0,2,1:T(8,128)S(1)}, u32[]{:S(2)}, u32[]{:S(2)}) collective-permute-start(f32[5,8,1,128]{3,0,2,1:T(8,128)S(1)} %slice.495), channel_id=1, source_target_pairs={{2,0},{3,1},{6,4},{7,5},{10,8},{11,9},{14,12},{15,13},{18,16},{19,... | collective-permute-start | bytes 61448 | tf_op jit(solution)/shard_map/ppermute | solution.py:42
  21.0 1.7 %collective-permute-done.2 = f32[5,8,1,128]{3,0,2,1:T(8,128)S(1)} collective-permute-done((f32[5,8,1,128]{3,0,2,1:T(8,128)S(1)}, f32[5,8,1,128]{3,0,2,1:T(8,128)S(1)}, u32[]{:S(2)}, u32[]{:S(2)}) %collective-permute-start.2) | collective-permute-done | bytes 20512 | tf_op jit(solution)/shard_map/ppermute | solution.py:42
  23.2 3.4 %collective-permute-start.5 = (f32[5,8,8,1]{3,0,2,1:T(8,128)S(1)}, f32[5,8,8,1]{3,0,2,1:T(8,128)S(1)}, u32[]{:S(2)}, u32[]{:S(2)}) collective-permute-start(f32[5,8,8,1]{3,0,2,1:T(8,128)S(1)} %slice.500), channel_id=1, source_target_pairs={{0,1},{2,3},{4,5},{6,7},{8,9},{10,11},{12,13},{14,15},{16,17},{18,... | collective-permute-start | bytes 3848 | tf_op jit(solution)/shard_map/ppermute | solution.py:42
  27.0 1.5 %collective-permute-start.4 = (f32[5,8,8,1]{3,0,2,1:T(8,128)S(1)}, f32[5,8,8,1]{3,0,2,1:T(8,128)S(1)}, u32[]{:S(2)}, u32[]{:S(2)}) collective-permute-start(f32[5,8,8,1]{3,0,2,1:T(8,128)S(1)} %bitcast.60), channel_id=1, source_target_pairs={{1,0},{3,2},{5,4},{7,6},{9,8},{11,10},{13,12},{15,14},{17,16},{19,... | collective-permute-start | bytes 3848 | tf_op jit(solution)/shard_map/ppermute | solution.py:42
  28.5 3.9 %collective-permute-done.5 = f32[5,8,8,1]{3,0,2,1:T(8,128)S(1)} collective-permute-done((f32[5,8,8,1]{3,0,2,1:T(8,128)S(1)}, f32[5,8,8,1]{3,0,2,1:T(8,128)S(1)}, u32[]{:S(2)}, u32[]{:S(2)}) %collective-permute-start.5) | collective-permute-done | bytes 1312 | tf_op jit(solution)/shard_map/ppermute | solution.py:42
  32.8 4.2 %collective-permute-done.4 = f32[5,8,8,1]{3,0,2,1:T(8,128)S(1)} collective-permute-done((f32[5,8,8,1]{3,0,2,1:T(8,128)S(1)}, f32[5,8,8,1]{3,0,2,1:T(8,128)S(1)}, u32[]{:S(2)}, u32[]{:S(2)}) %collective-permute-start.4) | collective-permute-done | bytes 1312 | tf_op jit(solution)/shard_map/ppermute | solution.py:42
  38.2 2.8 %multiply_reduce_fusion.1 = (f32[8,8,128]{2,1,0:T(8,128)S(1)}, f32[8,8,128]{2,1,0:T(8,128)S(1)}, f32[8,8,128]{2,1,0:T(8,128)S(1)}, f32[8,8,128]{2,1,0:T(8,128)S(...) fusion(f32[19,8,8,128]{3,0,2,1:T(8,128)} %constant.162, f32[19,8,8,128]{3,0,2,1:T(8,128)S(1)} %stack.50, ...), kind=kOutput, calls=%fused_computation.51 | convolution fusion | flops 39657472 | bytes 3335664 | tf_op jit(solution)/shard_map/transpose(jvp())/dot_general | solution.py:120
  43.6 1.3 %multiply_reduce_fusion.9 = (f32[]{:T(128)}, f32[8,8,128]{2,1,0:T(8,128)}, f32[8,8,128]{2,1,0:T(8,128)S(1)}, f32[8,8,128]{2,1,0:T(8,128)}, f32[8,8,128]{2,1,0:T(8,128)S(1)}) fusion(f32[8,8,128]{2,1,0:T(8,128)S(1)} %get-tuple-element.30, f32[8,8,128]{2,1,0:T(8,128)S(1)} %get-tuple-element.16, pred[8,8,128]{2,1,0:T(8,128)(4,1)S(1)} %get-tuple-element.39, ...), kind=kLoop, calls=%fused_computation.179 | loop fusion | flops 106495 | bytes 335908 | tf_op jit(solution)/shard_map/reduce_sum | solution.py:145
  44.9 2.2 %fusion.1 = f32[19,8,8,128]{3,0,2,1:T(8,128)S(1)} fusion(f32[3,19,1,1]{1,0,3,2:T(4,128)S(1)} %copy-done.18, f32[19,8,8,128]{3,0,2,1:T(8,128)S(1)} %get-tuple-element.177, f32[1,8,8,128]{3,0,2,1:T(1,128)S(1)} %get-tuple-element.84, f32[1,8,8,128]{3,0,2,1:T(1,128)S(1)} %get-tuple-element.85, f32[1,8,8,128]{3,0,2,1:T(1,128)S(1)} %get-tuple-element.86, ...), kind=kOutput, calls=%fused_computation.3 | convolution fusion | flops 9854976 | bytes 2679031 | tf_op jit(solution)/shard_map/transpose(jvp())/dot_general | solution.py:117
  47.9 4.4 %collective-permute-start.7 = (f32[5,1,8,128]{3,0,2,1:T(8,128)S(1)}, f32[5,1,8,128]{3,0,2,1:T(8,128)S(1)}, u32[]{:S(2)}, u32[]{:S(2)}) collective-permute-start(f32[5,1,8,128]{3,0,2,1:T(8,128)S(1)} %slice.515), channel_id=1, source_target_pairs={{0,4},{4,8},{8,12},{12,16},{16,20},{20,24},{24,28},{1,5},{5,9},{9,... | collective-permute-start | bytes 61448 | tf_op jit(solution)/shard_map/ppermute | solution.py:42
  54.1 4.4 %collective-permute-done.6 = f32[5,1,8,128]{3,0,2,1:T(8,128)S(1)} collective-permute-done((f32[5,1,8,128]{3,0,2,1:T(8,128)S(1)}, f32[5,1,8,128]{3,0,2,1:T(8,128)S(1)}, u32[]{:S(2)}, u32[]{:S(2)}) %collective-permute-start.6) | collective-permute-done | bytes 20512 | tf_op jit(solution)/shard_map/ppermute | solution.py:42
  64.0 1.7 %collective-permute-done.8 = f32[5,8,1,128]{3,0,2,1:T(8,128)S(1)} collective-permute-done((f32[5,8,1,128]{3,0,2,1:T(8,128)S(1)}, f32[5,8,1,128]{3,0,2,1:T(8,128)S(1)}, u32[]{:S(2)}, u32[]{:S(2)}) %collective-permute-start.8) | collective-permute-done | bytes 20512 | tf_op jit(solution)/shard_map/ppermute | solution.py:42
  66.2 1.5 %collective-permute-start.11 = (f32[5,8,8,1]{3,0,2,1:T(8,128)S(1)}, f32[5,8,8,1]{3,0,2,1:T(8,128)S(1)}, u32[]{:S(2)}, u32[]{:S(2)}) collective-permute-start(f32[5,8,8,1]{3,0,2,1:T(8,128)S(1)} %slice.531), channel_id=1, source_target_pairs={{0,1},{2,3},{4,5},{6,7},{8,9},{10,11},{12,13},{14,15},{16,17},{18,... | collective-permute-start | bytes 3848 | tf_op jit(solution)/shard_map/ppermute | solution.py:42
  68.1 1.5 %collective-permute-start.10 = (f32[5,8,8,1]{3,0,2,1:T(8,128)S(1)}, f32[5,8,8,1]{3,0,2,1:T(8,128)S(1)}, u32[]{:S(2)}, u32[]{:S(2)}) collective-permute-start(f32[5,8,8,1]{3,0,2,1:T(8,128)S(1)} %bitcast.61), channel_id=1, source_target_pairs={{1,0},{3,2},{5,4},{7,6},{9,8},{11,10},{13,12},{15,14},{17,16},{19,... | collective-permute-start | bytes 3848 | tf_op jit(solution)/shard_map/ppermute | solution.py:42
  69.7 4.0 %collective-permute-done.11 = f32[5,8,8,1]{3,0,2,1:T(8,128)S(1)} collective-permute-done((f32[5,8,8,1]{3,0,2,1:T(8,128)S(1)}, f32[5,8,8,1]{3,0,2,1:T(8,128)S(1)}, u32[]{:S(2)}, u32[]{:S(2)}) %collective-permute-start.11) | collective-permute-done | bytes 1312 | tf_op jit(solution)/shard_map/ppermute | solution.py:42
  74.1 4.2 %collective-permute-done.10 = f32[5,8,8,1]{3,0,2,1:T(8,128)S(1)} collective-permute-done((f32[5,8,8,1]{3,0,2,1:T(8,128)S(1)}, f32[5,8,8,1]{3,0,2,1:T(8,128)S(1)}, u32[]{:S(2)}, u32[]{:S(2)}) %collective-permute-start.10) | collective-permute-done | bytes 1312 | tf_op jit(solution)/shard_map/ppermute | solution.py:42
  79.5 2.8 %multiply_reduce_fusion = (f32[8,8,128]{2,1,0:T(8,128)S(1)}, f32[8,8,128]{2,1,0:T(8,128)S(1)}, f32[8,8,128]{2,1,0:T(8,128)S(1)}, f32[8,8,128]{2,1,0:T(8,128)S(1)...) fusion(f32[19,8,8,128]{3,0,2,1:T(8,128)} %constant.162, f32[19,8,8,128]{3,0,2,1:T(8,128)S(1)} %stack.57, ...), kind=kOutput, calls=%fused_computation.40 | convolution fusion | flops 39657472 | bytes 3335664 | tf_op jit(solution)/shard_map/transpose(jvp())/dot_general | solution.py:120
  83.3 1.6 %multiply_reduce_fusion.2 = (f32[8,8,128]{2,1,0:T(8,128)S(1)}, f32[8,8,128]{2,1,0:T(8,128)S(1)}, f32[3,8,8,128]{3,0,2,1:T(4,128)}) fusion(f32[3,8,8,128]{3,0,2,1:T(4,128)S(1)} %fusion.28, f32[8,8,128]{2,1,0:T(8,128)S(1)} %get-tuple-element.16, f32[8,8,128]{2,1,0:T(8,128)S(1)} %get-tuple-element.166, f32[8,8,128]{2,1,0:T(8,128)S(1)} %fusion.98, ...), kind=kOutput, calls=%fused_computation.106 | convolution fusion | flops 7340032 | bytes 1704240 | tf_op jit(solution)/shard_map/transpose(jvp())/dot_general | solution.py:103
  86.8 5.1 %all-to-all-start = ((f32[32,1,128]{2,1,0:T(1,128)}), f32[32,1,128]{2,1,0:T(1,128)S(1)}, u32[]{:S(2)}, u32[]{:S(2)}) async-start(f32[32,1,128]{2,1,0:T(1,128)} %iota.13), calls=%async_computation | async-start | bytes 32768 | tf_op jit(solution)/shard_map/all_to_all | solution.py:203
  92.6 2.2 %fusion = f32[19,8,8,128]{3,0,2,1:T(8,128)S(1)} fusion(f32[3,19,1,1]{1,0,3,2:T(4,128)S(1)} %copy-done.19, f32[19,8,8,128]{3,0,2,1:T(8,128)S(1)} %copy-done.27, f32[1,8,8,128]{3,0,2,1:T(1,128)S(1)} %get-tuple-element.47, f32[1,8,8,128]{3,0,2,1:T(1,128)S(1)} %get-tuple-element.48, f32[1,8,8,128]{3,0,2,1:T(1,128)S(1)} %get-tuple-element.49, ...), kind=kOutput, calls=%fused_computation.1 | convolution fusion | flops 9854976 | bytes 2679031 | tf_op jit(solution)/shard_map/transpose(jvp())/dot_general | solution.py:117
  95.8 3.3 %all-to-all-done = f32[32,1,128]{2,1,0:T(1,128)S(1)} async-done(((f32[32,1,128]{2,1,0:T(1,128)}), f32[32,1,128]{2,1,0:T(1,128)S(1)}, u32[]{:S(2)}, u32[]{:S(2)}) %all-to-all-start) | async-done | bytes 16416 | tf_op jit(solution)/shard_map/all_to_all | solution.py:203
  (146 shorter events, 29.5 us)
Async XLA Ops:
  0.6 10.3 %copy-start = (f32[2,19,8,8,128]{4,3,2,1,0:T(8,128)S(1)}, f32[2,19,8,8,128]{4,3,2,1,0:T(8,128)}, u32[]{:S(2)}) copy-start(f32[2,19,8,8,128]{4,3,2,1,0:T(8,128)} %param.22) | copy-start | bytes 3735556
  3.3 12.0 %collective-permute-start.1 = (f32[5,1,8,128]{3,0,2,1:T(8,128)}, f32[5,1,8,128]{3,0,2,1:T(8,128)}, u32[]{:S(2)}, u32[]{:S(2)}) collective-permute-start(f32[5,1,8,128]{3,0,2,1:T(8,128)} %slice.492), channel_id=1, source_target_pairs={{0,4},{4,8},{8,12},{12,16},{16,20},{20,24},{24,28},{1,5},{5,9},{9,... | collective-permute-start | bytes 61448 | tf_op jit(solution)/shard_map/ppermute | solution.py:42
  9.7 6.7 %collective-permute-start = (f32[5,1,8,128]{3,0,2,1:T(8,128)}, f32[5,1,8,128]{3,0,2,1:T(8,128)}, u32[]{:S(2)}, u32[]{:S(2)}) collective-permute-start(f32[5,1,8,128]{3,0,2,1:T(8,128)} %slice.491), channel_id=1, source_target_pairs={{4,0},{8,4},{12,8},{16,12},{20,16},{24,20},{28,24},{5,1},{9,5},{13... | collective-permute-start | bytes 61448 | tf_op jit(solution)/shard_map/ppermute | solution.py:42
  15.2 67.1 %copy-start.13 = (pred[8,8,128]{2,1,0:T(8,128)(4,1)}, pred[8,8,128]{2,1,0:T(8,128)(4,1)S(1)}, u32[]{:S(2)}) copy-start(pred[8,8,128]{2,1,0:T(8,128)(4,1)S(1)} %get-tuple-element.170) | copy-start | bytes 24580
  15.2 67.1 %copy-start.15 = (pred[8,8,128]{2,1,0:T(8,128)(4,1)}, pred[8,8,128]{2,1,0:T(8,128)(4,1)S(1)}, u32[]{:S(2)}) copy-start(pred[8,8,128]{2,1,0:T(8,128)(4,1)S(1)} %get-tuple-element.171) | copy-start | bytes 24580
  17.7 3.1 %collective-permute-start.3 = (f32[5,8,1,128]{3,0,2,1:T(8,128)S(1)}, f32[5,8,1,128]{3,0,2,1:T(8,128)S(1)}, u32[]{:S(2)}, u32[]{:S(2)}) collective-permute-start(f32[5,8,1,128]{3,0,2,1:T(8,128)S(1)} %slice.496), channel_id=1, source_target_pairs={{0,2},{1,3},{4,6},{5,7},{8,10},{9,11},{12,14},{13,15},{16,18},{17,... | collective-permute-start | bytes 61448 | tf_op jit(solution)/shard_map/ppermute | solution.py:42
  19.6 3.1 %collective-permute-start.2 = (f32[5,8,1,128]{3,0,2,1:T(8,128)S(1)}, f32[5,8,1,128]{3,0,2,1:T(8,128)S(1)}, u32[]{:S(2)}, u32[]{:S(2)}) collective-permute-start(f32[5,8,1,128]{3,0,2,1:T(8,128)S(1)} %slice.495), channel_id=1, source_target_pairs={{2,0},{3,1},{6,4},{7,5},{10,8},{11,9},{14,12},{15,13},{18,16},{19,... | collective-permute-start | bytes 61448 | tf_op jit(solution)/shard_map/ppermute | solution.py:42
  23.2 9.3 %collective-permute-start.5 = (f32[5,8,8,1]{3,0,2,1:T(8,128)S(1)}, f32[5,8,8,1]{3,0,2,1:T(8,128)S(1)}, u32[]{:S(2)}, u32[]{:S(2)}) collective-permute-start(f32[5,8,8,1]{3,0,2,1:T(8,128)S(1)} %slice.500), channel_id=1, source_target_pairs={{0,1},{2,3},{4,5},{6,7},{8,9},{10,11},{12,13},{14,15},{16,17},{18,... | collective-permute-start | bytes 3848 | tf_op jit(solution)/shard_map/ppermute | solution.py:42
  27.0 10.0 %collective-permute-start.4 = (f32[5,8,8,1]{3,0,2,1:T(8,128)S(1)}, f32[5,8,8,1]{3,0,2,1:T(8,128)S(1)}, u32[]{:S(2)}, u32[]{:S(2)}) collective-permute-start(f32[5,8,8,1]{3,0,2,1:T(8,128)S(1)} %bitcast.60), channel_id=1, source_target_pairs={{1,0},{3,2},{5,4},{7,6},{9,8},{11,10},{13,12},{15,14},{17,16},{19,... | collective-permute-start | bytes 3848 | tf_op jit(solution)/shard_map/ppermute | solution.py:42
  32.8 5.4 %copy-start.20 = (f32[19,19,1,1]{0,1,3,2:T(8,128)S(1)}, f32[19,19,1,1]{0,1,3,2:T(8,128)}, u32[]{:S(2)}) copy-start(f32[19,19,1,1]{0,1,3,2:T(8,128)} %constant.163) | copy-start | bytes 4336
  47.9 6.0 %collective-permute-start.7 = (f32[5,1,8,128]{3,0,2,1:T(8,128)S(1)}, f32[5,1,8,128]{3,0,2,1:T(8,128)S(1)}, u32[]{:S(2)}, u32[]{:S(2)}) collective-permute-start(f32[5,1,8,128]{3,0,2,1:T(8,128)S(1)} %slice.515), channel_id=1, source_target_pairs={{0,4},{4,8},{8,12},{12,16},{16,20},{20,24},{24,28},{1,5},{5,9},{9,... | collective-permute-start | bytes 61448 | tf_op jit(solution)/shard_map/ppermute | solution.py:42
  52.6 5.8 %collective-permute-start.6 = (f32[5,1,8,128]{3,0,2,1:T(8,128)S(1)}, f32[5,1,8,128]{3,0,2,1:T(8,128)S(1)}, u32[]{:S(2)}, u32[]{:S(2)}) collective-permute-start(f32[5,1,8,128]{3,0,2,1:T(8,128)S(1)} %slice.509), channel_id=1, source_target_pairs={{4,0},{8,4},{12,8},{16,12},{20,16},{24,20},{28,24},{5,1},{9,5},{13... | collective-permute-start | bytes 61448 | tf_op jit(solution)/shard_map/ppermute | solution.py:42
  58.8 5.1 %collective-permute-start.9 = (f32[5,8,1,128]{3,0,2,1:T(8,128)S(1)}, f32[5,8,1,128]{3,0,2,1:T(8,128)S(1)}, u32[]{:S(2)}, u32[]{:S(2)}) collective-permute-start(f32[5,8,1,128]{3,0,2,1:T(8,128)S(1)} %slice.525), channel_id=1, source_target_pairs={{0,2},{1,3},{4,6},{5,7},{8,10},{9,11},{12,14},{13,15},{16,18},{17,... | collective-permute-start | bytes 61448 | tf_op jit(solution)/shard_map/ppermute | solution.py:42
  62.6 3.1 %collective-permute-start.8 = (f32[5,8,1,128]{3,0,2,1:T(8,128)S(1)}, f32[5,8,1,128]{3,0,2,1:T(8,128)S(1)}, u32[]{:S(2)}, u32[]{:S(2)}) collective-permute-start(f32[5,8,1,128]{3,0,2,1:T(8,128)S(1)} %slice.521), channel_id=1, source_target_pairs={{2,0},{3,1},{6,4},{7,5},{10,8},{11,9},{14,12},{15,13},{18,16},{19,... | collective-permute-start | bytes 61448 | tf_op jit(solution)/shard_map/ppermute | solution.py:42
  66.2 7.5 %collective-permute-start.11 = (f32[5,8,8,1]{3,0,2,1:T(8,128)S(1)}, f32[5,8,8,1]{3,0,2,1:T(8,128)S(1)}, u32[]{:S(2)}, u32[]{:S(2)}) collective-permute-start(f32[5,8,8,1]{3,0,2,1:T(8,128)S(1)} %slice.531), channel_id=1, source_target_pairs={{0,1},{2,3},{4,5},{6,7},{8,9},{10,11},{12,13},{14,15},{16,17},{18,... | collective-permute-start | bytes 3848 | tf_op jit(solution)/shard_map/ppermute | solution.py:42
  68.1 10.1 %collective-permute-start.10 = (f32[5,8,8,1]{3,0,2,1:T(8,128)S(1)}, f32[5,8,8,1]{3,0,2,1:T(8,128)S(1)}, u32[]{:S(2)}, u32[]{:S(2)}) collective-permute-start(f32[5,8,8,1]{3,0,2,1:T(8,128)S(1)} %bitcast.61), channel_id=1, source_target_pairs={{1,0},{3,2},{5,4},{7,6},{9,8},{11,10},{13,12},{15,14},{17,16},{19,... | collective-permute-start | bytes 3848 | tf_op jit(solution)/shard_map/ppermute | solution.py:42
  74.0 5.4 %copy-start.11 = (f32[8,8,128]{2,1,0:T(8,128)S(1)}, f32[8,8,128]{2,1,0:T(8,128)}, u32[]{:S(2)}) copy-start(f32[8,8,128]{2,1,0:T(8,128)} %get-tuple-element.167) | copy-start | bytes 98308
  84.9 7.7 %copy-start.14 = (pred[8,8,128]{2,1,0:T(8,128)(4,1)S(1)}, pred[8,8,128]{2,1,0:T(8,128)(4,1)}, u32[]{:S(2)}) copy-start(pred[8,8,128]{2,1,0:T(8,128)(4,1)} %copy-done.13) | copy-start | bytes 24580
  84.9 7.7 %copy-start.16 = (pred[8,8,128]{2,1,0:T(8,128)(4,1)S(1)}, pred[8,8,128]{2,1,0:T(8,128)(4,1)}, u32[]{:S(2)}) copy-start(pred[8,8,128]{2,1,0:T(8,128)(4,1)} %copy-done.15) | copy-start | bytes 24580
  84.9 7.7 %copy-start.19 = (f32[3,19,1,1]{1,0,3,2:T(4,128)S(1)}, f32[3,19,1,1]{1,0,3,2:T(4,128)}, u32[]{:S(2)}) copy-start(f32[3,19,1,1]{1,0,3,2:T(4,128)} %constant.164) | copy-start | bytes 688
  84.9 7.7 %copy-start.23 = (pred[19]{0:T(512)(128)(4,1)S(1)}, pred[19]{0:T(512)(128)(4,1)}, u32[]{:S(2)}) copy-start(pred[19]{0:T(512)(128)(4,1)} %constant.60.clone.1) | copy-start | bytes 61
  84.9 7.7 %copy-start.27 = (f32[19,8,8,128]{3,0,2,1:T(8,128)S(1)}, f32[19,8,8,128]{3,0,2,1:T(8,128)}, u32[]{:S(2)}) copy-start(f32[19,8,8,128]{3,0,2,1:T(8,128)} %copy-done.26) | copy-start | bytes 1867780
  84.9 7.7 %copy-start.28 = (f32[3,8,8,128]{3,0,2,1:T(4,128)S(1)}, f32[3,8,8,128]{3,0,2,1:T(4,128)}, u32[]{:S(2)}) copy-start(f32[3,8,8,128]{3,0,2,1:T(4,128)} %get-tuple-element.180) | copy-start | bytes 294916
  86.8 12.3 %all-to-all-start = ((f32[32,1,128]{2,1,0:T(1,128)}), f32[32,1,128]{2,1,0:T(1,128)S(1)}, u32[]{:S(2)}, u32[]{:S(2)}) async-start(f32[32,1,128]{2,1,0:T(1,128)} %iota.13), calls=%async_computation | async-start | bytes 32768 | tf_op jit(solution)/shard_map/all_to_all | solution.py:203
  (18 other events, 53.7 us)

commit v2 on v0

v2 whole, which is shorter than its diff:
```python
from functools import partial

import jax
import jax.numpy as jnp
import numpy as np
from jax import lax
from jax.experimental import pallas as pl
from jax.experimental.pallas import tpu as pltpu
from jax.sharding import PartitionSpec as P

lattice = [
    (0, 0, 0), (1, 0, 0), (-1, 0, 0), (0, 1, 0), (0, -1, 0), (0, 0, 1), (0, 0, -1),
    (1, 1, 0), (-1, -1, 0), (1, -1, 0), (-1, 1, 0), (1, 0, 1), (-1, 0, -1),
    (1, 0, -1), (-1, 0, 1), (0, 1, 1), (0, -1, -1), (0, 1, -1), (0, -1, 1),
]
axes = ("gx", "gy", "gz")
brinkman_max = 4.0
convexity = 0.1
inflow_speed = 0.08
ups = [[i for i in range(19) if lattice[i][d] == 1] for d in range(3)]
downs = [[i for i in range(19) if lattice[i][d] == -1] for d in range(3)]


def relax_factors():
    c = np.array(lattice, np.float64)
    cx, cy, cz = c[:, 0], c[:, 1], c[:, 2]
    q = (c * c).sum(1)
    shear = 1.0 / 0.6
    rows = {
        "E": (19 * q - 30, 1.19),
        "S": ((21 * q * q - 53 * q + 24) / 2, 1.4),
        "Q": ((5 * q - 9) * cx, 1.2),
        "P": (3 * cx * cx - q, shear),
        "PP": ((3 * q - 5) * (3 * cx * cx - q), 1.4),
        "W": (cy * cy - cz * cz, shear),
        "WW": ((3 * q - 5) * (cy * cy - cz * cz), 1.4),
        "C": (cx * cy, shear),
        "M": ((cy * cy - cz * cz) * cx, 1.98),
    }
    return {k: float(rate / (row * row).sum()) for k, (row, rate) in rows.items()}


factor = relax_factors()


def flow_of(d, g):
    rho = d[0]
    for i in range(1, 19):
        rho = rho + d[i]
    o7, o9, o11, o13, o15, o17 = (d[k] - d[k + 1] for k in (7, 9, 11, 13, 15, 17))
    jx = (d[1] - d[2]) + ((o7 + o9) + (o11 + o13))
    jy = (d[3] - d[4]) + ((o7 - o9) + (o15 + o17))
    jz = (d[5] - d[6]) + ((o11 - o13) + (o15 - o17))
    mixed = brinkman_max * convexity
    iden = 1.0 / ((convexity + mixed) + (1.0 - mixed) * g)
    irho = 1.0 / rho
    damp = (convexity + g) * iden
    slope = (mixed * (1.0 + convexity)) * (iden * iden)
    beta = damp * irho
    return rho, irho, jx * beta, jy * beta, jz * beta, beta, (jx * irho, jy * irho, jz * irho), slope


def local_adjoint(p, flow, solid, kind, wt):
    rho, irho, ux, uy, uz, beta = flow[:6]
    is_solid = solid == 1
    fluid = solid == 0
    inlet = kind == 1
    outlet = kind == 2
    pairs = (1, 3, 5, 7, 9, 11, 13, 15, 17)
    he = {k: 0.5 * (p[k] + p[k + 1]) for k in pairs}
    ho = {k: 0.5 * (p[k] - p[k + 1]) for k in pairs}
    xy, xz, yz = he[7] + he[9], he[11] + he[13], he[15] + he[17]
    ax = he[1] + he[3] + he[5]
    dg = xy + xz + yz
    e_m = (-30.0 * p[0] - 22.0 * ax + 16.0 * dg) * factor["E"]
    s_m = (12.0 * p[0] - 8.0 * ax + 2.0 * dg) * factor["S"]
    pa = 3.0 * he[1] - ax
    pd = dg - 3.0 * yz
    a1 = (2.0 * factor["P"]) * (pa + pd)
    a2 = (2.0 * factor["PP"]) * (pd - 2.0 * pa)
    wa, wd = he[3] - he[5], xy - xz
    b1 = (2.0 * factor["W"]) * (wa + wd)
    b2 = (2.0 * factor["WW"]) * (wd - 2.0 * wa)
    cxy = (2.0 * factor["C"]) * (he[7] - he[9])
    cxz = (2.0 * factor["C"]) * (he[11] - he[13])
    cyz = (2.0 * factor["C"]) * (he[15] - he[17])
    r0 = 12.0 * s_m - 30.0 * e_m
    ca = -11.0 * e_m - 4.0 * s_m
    cd = 8.0 * e_m + s_m
    a12, b12 = a1 - 2.0 * a2, b1 - 2.0 * b2
    t = ca - a12
    aa, bb = a1 + a2, b1 + b2
    dxy, dxz, dyz = cd + aa + bb, cd + aa - bb, cd - 2.0 * aa
    re = {
        1: ca + 2.0 * a12, 3: t + b12, 5: t - b12,
        7: dxy + cxy, 9: dxy - cxy, 11: dxz + cxz, 13: dxz - cxz, 15: dyz + cyz, 17: dyz - cyz,
    }
    xa, xb = ho[7] + ho[9], ho[11] + ho[13]
    ya, yb = ho[7] - ho[9], ho[15] + ho[17]
    za, zb = ho[11] - ho[13], ho[15] - ho[17]
    fq, fm = 2.0 * factor["Q"], 2.0 * factor["M"]
    qx, qy, qz = ((s - 4.0 * o) * fq for s, o in ((xa + xb, ho[1]), (ya + yb, ho[3]), (za + zb, ho[5])))
    mx, my, mz = (xa - xb) * fm, (yb - ya) * fm, (za - zb) * fm
    x1, x2 = qx + mx, qx - mx
    y1, y2 = qy - my, qy + my
    z1, z2 = qz + mz, qz - mz
    ro = {
        1: -4.0 * qx, 3: -4.0 * qy, 5: -4.0 * qz,
        7: x1 + y1, 9: x1 - y1, 11: x2 + z1, 13: x2 - z1, 15: y2 + z2, 17: y2 - z2,
    }
    v0 = jnp.where(outlet, p[0], r0)
    ve = {k: jnp.where(outlet, he[k], re[k]) for k in pairs}
    vo = {k: jnp.where(outlet, ho[k], ro[k]) for k in pairs}
    n, d = 1.0 / 9.0, 1.0 / 18.0
    vxy, vxz, vyz = ve[7] + ve[9], ve[11] + ve[13], ve[15] + ve[17]
    s0 = v0 * (1.0 / 3.0) + n * (ve[1] + ve[3] + ve[5]) + d * (vxy + vxz + vyz)
    s1x = n * vo[1] + d * ((vo[7] + vo[9]) + (vo[11] + vo[13]))
    s1y = n * vo[3] + d * ((vo[7] - vo[9]) + (vo[15] + vo[17]))
    s1z = n * vo[5] + d * ((vo[11] - vo[13]) + (vo[15] - vo[17]))
    sxx = n * ve[1] + d * (vxy + vxz)
    syy = n * ve[3] + d * (vxy + vyz)
    szz = n * ve[5] + d * (vxz + vyz)
    sxy, sxz, syz = d * (ve[7] - ve[9]), d * (ve[11] - ve[13]), d * (ve[15] - ve[17])
    vx = sxx * ux + sxy * uy + sxz * uz
    vy = sxy * ux + syy * uy + syz * uz
    vz = sxz * ux + syz * uy + szz * uz
    usq = ux * ux + uy * uy + uz * uz
    along = ux * s1x + uy * s1y + uz * s1z
    bend = ux * vx + uy * vy + uz * vz
    d_rho = s0 + 3.0 * along + 4.5 * bend - 1.5 * usq * s0
    us = inflow_speed
    base = 1.0 - 1.5 * us * us
    full = base + 4.5 * us * us
    q_in = (
        (base / 3.0) * p[0] + (n * full) * he[1] + (n * 3.0 * us) * ho[1] + (n * base) * (he[3] + he[5])
        + (d * full) * (xy + xz) + (d * 3.0 * us) * (xa + xb) + (d * base) * yz
    )
    scale = jnp.where(inlet, 0.0, jnp.where(outlet, 1.0, rho))
    kin = wt * rho
    lx = scale * (3.0 * s1x + 9.0 * vx - 3.0 * ux * s0) + kin * ux
    ly = scale * (3.0 * s1y + 9.0 * vy - 3.0 * uy * s0) + kin * uy
    lz = scale * (3.0 * s1z + 9.0 * vz - 3.0 * uz * s0) + kin * uz
    r = jnp.where(inlet, q_in, jnp.where(outlet, 0.0, d_rho)) + 0.5 * wt * usq
    r = r - (lx * ux + ly * uy + lz * uz) * irho
    r = jnp.where(is_solid, 0.0, r)
    bs = jnp.where(is_solid, 0.0, beta)
    gx, gy, gz = lx * bs, ly * bs, lz * bs
    inside = jnp.logical_not(is_solid | inlet | outlet)
    on = jnp.where(inside, 1.0, 0.0)
    keep = jnp.where(is_solid, 1.0, on)
    flip = jnp.where(is_solid, -1.0, on)
    out = [None] * 19
    out[0] = r + keep * p[0] - on * r0
    flux = {1: gx, 3: gy, 5: gz, 7: gx + gy, 9: gx - gy, 11: gx + gz, 13: gx - gz, 15: gy + gz, 17: gy - gz}
    for k in pairs:
        even = r + (keep * he[k] - on * re[k])
        odd = flux[k] + (flip * ho[k] - on * ro[k])
        out[k] = even + odd
        out[k + 1] = even - odd
    cost = jnp.where(fluid, 0.5 * kin * usq, 0.0)
    return out, (lx, ly, lz), cost


def swap_pairs(size, odd):
    if not odd:
        return [(i, i ^ 1) for i in range(size)]
    inner = [(i, i + 1 if i % 2 else i - 1) for i in range(1, size - 1)]
    return [(0, 0)] + inner + [(size - 1, size - 1)]


class Link:
    def __init__(self, axis, size):
        assert size % 2 == 0
        self.axis, self.size = axis, size
        self.count = 1 if size == 2 else 2

    def swap(self, messages):
        return [lax.ppermute(m, self.axis, swap_pairs(self.size, k)) for k, m in enumerate(messages)]

    def emit(self, refs, slot, up, down):
        even = lax.axis_index(self.axis) % 2 == 0
        refs[0][slot] = jnp.where(even, up, down)
        if self.count == 2:
            refs[1][slot] = jnp.where(even, down, up)

    def ends(self):
        at = lax.axis_index(self.axis)
        return at == 0, at == self.size - 1

    def above(self, refs, slot):
        even = lax.axis_index(self.axis) % 2 == 0
        value = refs[0][slot]
        if self.count == 2:
            value = jnp.where(even, value, refs[1][slot])
        return jnp.where(self.ends()[1], 0.0, value)

    def below(self, refs, slot):
        even = lax.axis_index(self.axis) % 2 == 0
        value = refs[0][slot]
        if self.count == 2:
            value = jnp.where(even, refs[1][slot], value)
        return jnp.where(self.ends()[0], 0.0, value)


def roll(tile, shift, axis):
    shift = shift % tile.shape[axis]
    return tile if shift == 0 else pltpu.roll(tile, shift, axis)


def iotas():
    return lax.broadcasted_iota(jnp.int32, (8, 128), 0), lax.broadcasted_iota(jnp.int32, (8, 128), 1)


def shift_y(tile, i, x, y_above, y_below, sub):
    cy = lattice[i][1]
    if cy == 0:
        return tile
    rows = y_above if cy == 1 else y_below
    k = (ups if cy == 1 else downs)[1].index(i)
    row = jnp.broadcast_to(rows[k][x : x + 1, :], (8, 128))
    return jnp.where(sub == (7 if cy == 1 else 0), row, roll(tile, -cy, 0))


def shift_z(tile, i, x, z_above, z_below, lane):
    cz = lattice[i][2]
    if cz == 0:
        return tile
    k = (ups if cz == 1 else downs)[2].index(i)
    at = 127 if cz == 1 else 0
    column = roll(z_above if cz == 1 else z_below, at - (k * 8 + x), 1)
    return jnp.where(lane == at, column, roll(tile, -cz, 1))


def y_rows(links, refs):
    return [links[1].above(refs, k) for k in range(5)], [links[1].below(refs, k) for k in range(5)]


def pack_y(links, a, out):
    for k in range(5):
        up = a[downs[1][k], :, 7, :]
        down = a[ups[1][k], :, 0, :]
        links[1].emit(out, k, up, down)


def pack_z(links, a, ys, out):
    sub, lane = iotas()
    y_above, y_below = y_rows(links, ys)
    even = lax.axis_index("gz") % 2 == 0
    up, down = jnp.zeros((8, 128), jnp.float32), jnp.zeros((8, 128), jnp.float32)
    for k in range(5):
        for x in range(8):
            at = k * 8 + x
            i, j = downs[2][k], ups[2][k]
            tile = roll(shift_y(a[i, x], i, x, y_above, y_below, sub), at - 127, 1)
            up = jnp.where(lane == at, tile, up)
            tile = roll(shift_y(a[j, x], j, x, y_above, y_below, sub), at, 1)
            down = jnp.where(lane == at, tile, down)
    links[2].emit(out, 0, up, down)


def pack_x(links, a, ys, zs, out):
    sub, lane = iotas()
    y_above, y_below = y_rows(links, ys)
    z_above, z_below = links[2].above(zs, 0), links[2].below(zs, 0)
    for k in range(5):
        both = []
        for i, x in ((downs[0][k], 7), (ups[0][k], 0)):
            tile = shift_y(a[i, x], i, x, y_above, y_below, sub)
            both.append(shift_z(tile, i, x, z_above, z_below, lane))
        links[0].emit(out, k, *both)


def pack_z_kernel(links, a, *refs):
    n = links[1].count
    pack_z(links, a, refs[:n], refs[n:])


def pack_x_kernel(links, a, *refs):
    n, m = links[1].count, links[2].count
    pack_x(links, a, refs[:n], refs[n : n + m], refs[n + m :])


def pack_y_kernel(links, a, *refs):
    pack_y(links, a, refs)


def step_kernel(links, whole_x, last, a, states, g, solid, kind, *refs):
    counts = [links[1].count, links[2].count, links[0].count]
    refs = list(refs)
    take = lambda n: [refs.pop(0) for _ in range(n)]
    ys, zs, xs = (take(c) for c in counts)
    if last:
        sens_in, cost_in = take(2)
    new, sens, cost = take(3)
    sub, lane = iotas()
    y_above, y_below = y_rows(links, ys)
    z_above, z_below = links[2].above(zs, 0), links[2].below(zs, 0)
    start = lax.axis_index("gx") * 8
    total = jnp.zeros((8, 128), jnp.float32)
    squares = jnp.zeros((8, 128), jnp.float32)
    for x in range(8):
        p = []
        for i in range(19):
            cx = lattice[i][0]
            if not 0 <= x + cx < 8:
                k = (ups if cx == 1 else downs)[0].index(i)
                p.append((links[0].above if cx == 1 else links[0].below)(xs, k))
                continue
            tile = shift_y(a[i, x + cx], i, x + cx, y_above, y_below, sub)
            p.append(shift_z(tile, i, x + cx, z_above, z_below, lane))
        d = [states[0 if last else 1, i, x] for i in range(19)]
        flow = flow_of(d, g[x])
        wt = 1.0 + 2.0 * (start + x).astype(jnp.float32) / (whole_x - 1)
        out, force, k_cell = local_adjoint(p, flow, solid[x], kind[x], wt)
        for i in range(19):
            new[i, x] = out[i]
        v = flow[6]
        s = (force[0] * v[0] + force[1] * v[1] + force[2] * v[2]) * flow[7]
        s = jnp.where(solid[x] == 1, 0.0, s)
        total = total + k_cell
        if last:
            s = s + sens_in[x]
            squares = squares + s * s
        sens[x] = s
    if last:
        total = jnp.sum(total + cost_in[...], axis=0, keepdims=True)
        squares = jnp.sum(squares, axis=0, keepdims=True)
        both = jnp.where(lane[:1] < 64, jnp.sum(total), jnp.sum(squares))
        cost[...] = jnp.broadcast_to(both[None], cost.shape)
    else:
        cost[...] = total
        pack_y(links, new, refs)


def finish_kernel(cells, got, sens, out, scalars):
    sums = jnp.sum(got[...], axis=0)
    cost = jnp.sum(sums[:, :1])
    square = jnp.sum(sums[:, 64:65])
    lane = lax.broadcasted_iota(jnp.int32, (1, 128), 1)
    rms = jnp.sqrt(jnp.broadcast_to(square / cells, (1, 128)) + 1e-06)
    out[...] = sens[...] / jnp.broadcast_to(rms[None], sens.shape)
    scalars[...] = jnp.where(lane < 64, jnp.broadcast_to(cost / cells, (1, 128)), rms)


vmem = pl.BlockSpec(memory_space=pltpu.VMEM)


def call(kernel, outs, *args, name):
    shapes = tuple(jax.ShapeDtypeStruct(s, jnp.float32) for s in outs)
    return pl.pallas_call(
        kernel, out_shape=shapes, in_specs=[vmem] * len(args), out_specs=tuple([vmem] * len(outs)), name=name
    )(*args)


def pull_messages(links, a, y_messages):
    ys = links[1].swap(y_messages)
    zs = call(partial(pack_z_kernel, links), [(1, 8, 128)] * links[2].count, a, *ys, name="pack_z")
    zs = links[2].swap(zs)
    xs = call(partial(pack_x_kernel, links), [(5, 8, 128)] * links[0].count, a, *ys, *zs, name="pack_x")
    xs = links[0].swap(xs)
    return (*ys, *zs, *xs)


def body(sizes, a, states, design, solid, kind):
    links = [Link(axis, sizes[axis]) for axis in axes]
    devices = sizes["gx"] * sizes["gy"] * sizes["gz"]
    assert design.shape == (8, 8, 128)
    cells = devices * design.size
    whole_x = sizes["gx"] * 8
    field = a.shape
    y_shapes = [(5, 8, 128)] * links[1].count
    ys = call(partial(pack_y_kernel, links), y_shapes, a, name="pack_y")
    messages = pull_messages(links, a, ys)
    a, sens, cost, *ys = call(
        partial(step_kernel, links, whole_x, False), [field, design.shape, (8, 128), *y_shapes],
        a, states, design, solid, kind, *messages, name="step_1",
    )
    messages = pull_messages(links, a, ys)
    a, sens, sums = call(
        partial(step_kernel, links, whole_x, True), [field, design.shape, (devices, 1, 128)],
        a, states, design, solid, kind, *messages, sens, cost, name="step_0",
    )
    got = lax.all_to_all(sums, axes, 0, 0)
    sens, scalars = call(partial(finish_kernel, cells), [design.shape, (1, 128)], got, sens, name="finish")
    return a, sens, scalars[0, 0], scalars[0, 64]


def solution(mesh):
    cell = P("gx", "gy", "gz")
    placed = (P(None, *cell), P(None, None, *cell), cell, cell, cell)
    return jax.shard_map(
        partial(body, dict(mesh.shape)),
        mesh=mesh,
        in_specs=placed,
        out_specs=(P(None, *cell), cell, P(), P()),
        check_vma=False,
    )
```

time: 135 us -> 62.2 us (0.46)
  blocking collectives: 40.5 us -> 17.4 us
  matrix products: 18 us -> 0 us
  waiting for transfers between devices: 24.1 us -> 7.26 us
  Pallas kernels: 0 us -> 16.5 us
  starting transfers between devices: 25.6 us -> 14.4 us
  other arithmetic: 7.97 us -> 0 us
  local copies, waits for them, and re-layouts: 11.4 us -> 5.46 us
  between operations: 6.56 us -> 0.65 us
    psum x1 -> x0, blocking collectives: 40.5 us -> none  [body(): lax.psum(jnp.sum(sens_total * sens_total), ('gx', 'gy', 'gz'))]
    dot_general x12 -> x0, matrix products: 18 us -> none  [the longest x6 6.21 us: equilibrium(): jnp.tensordot(velocity_table, velocity, axes=(1, 0), precision=lax.Precis...]
    all_to_all x0 -> x1, blocking collectives: none -> 17.4 us  [body(): got = lax.all_to_all(sums, axes, 0, 0)]
    ppermute x12 -> x8, waiting for transfers between devices: 24.1 us -> 7.26 us  [swap(): lax.ppermute(m, self.axis, swap_pairs(self.size, k))]
    pallas_call x0 -> x8, Pallas kernels: none -> 16.5 us  [call(): pl.pallas_call(kernel, out_shape=shapes, in_specs=[vmem] * len(args), out...]
    ppermute x12 -> x8, starting transfers between devices: 25.6 us -> 14.4 us  [swap(): lax.ppermute(m, self.axis, swap_pairs(self.size, k))]
    another operation x16 -> x0, local copies, waits for them, and re-layouts: 5.46 us -> none  [the longest x2 1.48 us: pull_directed(): return jnp.stack(pieces)]
    concatenate x12 -> x0, other arithmetic: 3.74 us -> none  [the longest x6 2.05 us: place_moving(): jnp.concatenate([lax.slice_in_dim(up_stack, 1, length, 1, dim), from_abov...]
  transfers between devices with their start and end apart: 12 -> 8, of which waited for: 7 -> 6; matrix products, arithmetic and copies ran while one was open for 7% -> 0% of each run, Pallas kernels for 0% -> 0%
where the time goes in v2:
time: 62.2 us; the launch traced here: 61.7 us
  blocking collectives  17.4 us (28%)
  Pallas kernels  16.5 us (27%)
  starting transfers between devices  14.4 us (23%)
  waiting for transfers between devices  7.26 us (12%)
  local copies, waits for them, and re-layouts  5.46 us (9%)
  between operations  0.65 us (1%)
    all_to_all x1, blocking collectives, body(): got = lax.all_to_all(sums, axes, 0, 0)  17.4 us
    pallas_call x8, Pallas kernels, call(): pl.pallas_call(kernel, out_shape=shapes, in_specs=[vmem] * len(args), out...  16.5 us
    ppermute x8, starting transfers between devices, swap(): lax.ppermute(m, self.axis, swap_pairs(self.size, k))  14.4 us
    ppermute x8, waiting for transfers between devices, swap(): lax.ppermute(m, self.axis, swap_pairs(self.size, k))  7.26 us
    unnamed x16, local copies, waits for them, and re-layouts  4.19 us
    slice x1, local copies, waits for them, and re-layouts, body(): return (a, sens, scalars[0, 0], scalars[0, 64])  1.27 us
  transfers between devices with their start and end apart: 8, of which 6 were waited for; matrix products, arithmetic and copies ran while one was open for 0% of the time, Pallas kernels for 0%

profile of v2, /device:TPU:0, one launch (start us, length us, event | category | flops | bytes accessed | tf_op | source)
XLA Modules:
  0.0 61.7 jit_solution(11831458168131356178)
XLA Ops:
  0.6 1.7 %pack_y.1 = f32[5,8,128]{2,1,0:T(8,128)} custom-call(f32[19,8,8,128]{3,2,1,0:T(8,128)} %a.7), custom_call_target="tpu_custom_call" | custom-call | tf_op jit(solution)/shard_map/pack_y/pallas_call | solution.py:350
  2.8 1.1 %collective-permute-done.refs_0_ = f32[5,8,128]{2,1,0:T(8,128)S(1)} collective-permute-done((f32[5,8,128]{2,1,0:T(8,128)}, f32[5,8,128]{2,1,0:T(8,128)S(1)}, u32[]{:S(2)}, u32[]{:S(2)}) %collective-permute-start) | collective-permute-done | bytes 20512 | tf_op jit(solution)/shard_map/ppermute | solution.py:178
  3.9 0.6 copy-done.1
  4.5 1.8 %pack_z.2 = f32[1,8,128]{2,1,0:T(8,128)} custom-call(f32[19,8,8,128]{3,2,1,0:T(8,128)} %a.7, f32[5,8,128]{2,1,0:T(8,128)} %copy-done.1), custom_call_target="tpu_custom_call" | custom-call | tf_op jit(solution)/shard_map/pack_z/pallas_call | solution.py:350
  6.3 2.8 %collective-permute-start.1 = (f32[1,8,128]{2,1,0:T(8,128)}, f32[1,8,128]{2,1,0:T(8,128)S(1)}, u32[]{:S(2)}, u32[]{:S(2)}) collective-permute-start(f32[1,8,128]{2,1,0:T(8,128)} %pack_z.2), channel_id=1, source_target_pairs={{0,1},{1,0},{2,3},{3,2},{4,5},{5,4},{6,7},{7,6},{8,9},{9,8},{10,11... | collective-permute-start | bytes 12296 | tf_op jit(solution)/shard_map/ppermute | solution.py:178
  9.1 1.8 %collective-permute-done.1.refs_1_ = f32[1,8,128]{2,1,0:T(8,128)S(1)} collective-permute-done((f32[1,8,128]{2,1,0:T(8,128)}, f32[1,8,128]{2,1,0:T(8,128)S(1)}, u32[]{:S(2)}, u32[]{:S(2)}) %collective-permute-start.1) | collective-permute-done | bytes 4128 | tf_op jit(solution)/shard_map/ppermute | solution.py:178
  11.5 1.8 %pack_x.2 = (f32[5,8,128]{2,1,0:T(8,128)}, f32[5,8,128]{2,1,0:T(8,128)}) custom-call(f32[19,8,8,128]{3,2,1,0:T(8,128)} %a.7, f32[5,8,128]{2,1,0:T(8,128)} %copy-done.1, f32[1,8,128]{2,1,0:T(8,128)} %copy-done.7), custom_call_target="tpu_custom_call" | custom-call | tf_op jit(solution)/shard_map/pack_x/pallas_call | solution.py:350
  13.3 2.1 %collective-permute-start.2 = (f32[5,8,128]{2,1,0:T(8,128)}, f32[5,8,128]{2,1,0:T(8,128)S(1)}, u32[]{:S(2)}, u32[]{:S(2)}) collective-permute-start(f32[5,8,128]{2,1,0:T(8,128)} %get-tuple-element.17), channel_id=1, source_target_pairs={{0,4},{4,0},{8,12},{12,8},{16,20},{20,16},{24,28},{28,24},{1,5},{5... | collective-permute-start | bytes 61448 | tf_op jit(solution)/shard_map/ppermute | solution.py:178
  15.4 1.4 %collective-permute-start.3 = (f32[5,8,128]{2,1,0:T(8,128)}, f32[5,8,128]{2,1,0:T(8,128)S(1)}, u32[]{:S(2)}, u32[]{:S(2)}) collective-permute-start(f32[5,8,128]{2,1,0:T(8,128)} %get-tuple-element.18), channel_id=1, source_target_pairs={{0,0},{4,8},{8,4},{12,16},{16,12},{20,24},{24,20},{28,28},{1,1},{5... | collective-permute-start | bytes 61448 | tf_op jit(solution)/shard_map/ppermute | solution.py:178
  17.9 0.6 copy-done.5
  18.5 3.0 %step_1.1 = (f32[19,8,8,128]{3,2,1,0:T(8,128)}, f32[8,8,128]{2,1,0:T(8,128)}, f32[8,128]{1,0:T(8,128)}, f32[5,8,128]{2,1,0:T(8,128)}) custom-call(f32[19,8,8,128]{3,2,1,0:T(8,128)} %a.7, f32[2,19,8,8,128]{4,3,2,1,0:T(8,128)} %states.3, f32[8,8,128]{2,1,0:T(8,128)} %g.3, s32[8,8,128]{2,1,0:T(8,128)} %solid.3, s32[8,8,128]{2,1,0:T(8,128)} %kind.3, ...), custom_call_target="tpu_custom_call" | custom-call | tf_op jit(solution)/shard_map/step_1/pallas_call | solution.py:350
  21.5 1.4 %collective-permute-done.4.refs_0_ = f32[5,8,128]{2,1,0:T(8,128)S(1)} collective-permute-done((f32[5,8,128]{2,1,0:T(8,128)}, f32[5,8,128]{2,1,0:T(8,128)S(1)}, u32[]{:S(2)}, u32[]{:S(2)}) %collective-permute-start.4) | collective-permute-done | bytes 20512 | tf_op jit(solution)/shard_map/ppermute | solution.py:178
  22.9 0.6 copy-done
  23.5 1.8 %pack_z.3 = f32[1,8,128]{2,1,0:T(8,128)} custom-call(f32[19,8,8,128]{3,2,1,0:T(8,128)} %get-tuple-element.19.a, f32[5,8,128]{2,1,0:T(8,128)} %copy-done), custom_call_target="tpu_custom_call" | custom-call | tf_op jit(solution)/shard_map/pack_z/pallas_call | solution.py:350
  25.4 2.0 %collective-permute-start.5 = (f32[1,8,128]{2,1,0:T(8,128)}, f32[1,8,128]{2,1,0:T(8,128)S(1)}, u32[]{:S(2)}, u32[]{:S(2)}) collective-permute-start(f32[1,8,128]{2,1,0:T(8,128)} %pack_z.3), channel_id=1, source_target_pairs={{0,1},{1,0},{2,3},{3,2},{4,5},{5,4},{6,7},{7,6},{8,9},{9,8},{10,11... | collective-permute-start | bytes 12296 | tf_op jit(solution)/shard_map/ppermute | solution.py:178
  27.4 1.8 %collective-permute-done.5.refs_1_ = f32[1,8,128]{2,1,0:T(8,128)S(1)} collective-permute-done((f32[1,8,128]{2,1,0:T(8,128)}, f32[1,8,128]{2,1,0:T(8,128)S(1)}, u32[]{:S(2)}, u32[]{:S(2)}) %collective-permute-start.5) | collective-permute-done | bytes 4128 | tf_op jit(solution)/shard_map/ppermute | solution.py:178
  29.8 1.8 %pack_x.3 = (f32[5,8,128]{2,1,0:T(8,128)}, f32[5,8,128]{2,1,0:T(8,128)}) custom-call(f32[19,8,8,128]{3,2,1,0:T(8,128)} %get-tuple-element.19.a, f32[5,8,128]{2,1,0:T(8,128)} %copy-done, f32[1,8,128]{2,1,0:T(8,128)} %copy-done.6), custom_call_target="tpu_custom_call" | custom-call | tf_op jit(solution)/shard_map/pack_x/pallas_call | solution.py:350
  31.5 4.3 %collective-permute-start.6 = (f32[5,8,128]{2,1,0:T(8,128)}, f32[5,8,128]{2,1,0:T(8,128)S(1)}, u32[]{:S(2)}, u32[]{:S(2)}) collective-permute-start(f32[5,8,128]{2,1,0:T(8,128)} %get-tuple-element.21), channel_id=1, source_target_pairs={{0,4},{4,0},{8,12},{12,8},{16,20},{20,16},{24,28},{28,24},{1,5},{5... | collective-permute-start | bytes 61448 | tf_op jit(solution)/shard_map/ppermute | solution.py:178
  35.9 1.4 %collective-permute-start.7 = (f32[5,8,128]{2,1,0:T(8,128)}, f32[5,8,128]{2,1,0:T(8,128)S(1)}, u32[]{:S(2)}, u32[]{:S(2)}) collective-permute-start(f32[5,8,128]{2,1,0:T(8,128)} %get-tuple-element.22), channel_id=1, source_target_pairs={{0,0},{4,8},{8,4},{12,16},{16,12},{20,24},{24,20},{28,28},{1,1},{5... | collective-permute-start | bytes 61448 | tf_op jit(solution)/shard_map/ppermute | solution.py:178
  37.3 0.6 collective-permute-done.6.refs_2_
  38.5 3.0 %step_0.1 = (f32[19,8,8,128]{3,2,1,0:T(8,128)}, f32[8,8,128]{2,1,0:T(8,128)}, f32[32,1,128]{2,1,0:T(1,128)}) custom-call(f32[19,8,8,128]{3,2,1,0:T(8,128)} %get-tuple-element.19.a, f32[2,19,8,8,128]{4,3,2,1,0:T(8,128)} %states.3, f32[8,8,128]{2,1,0:T(8,128)} %g.3, s32[8,8,128]{2,1,0:T(8,128)} %solid.3, s32[8,8,128]{2,1,0:T(8,128)} %kind.3, ...), custom_call_target="tpu_custom_call" | custom-call | tf_op jit(solution)/shard_map/step_0/pallas_call | solution.py:350
  41.5 17.4 %all_to_all.5.got = f32[32,1,128]{2,1,0:T(1,128)} all-to-all(f32[32,1,128]{2,1,0:T(1,128)} %get-tuple-element.26), channel_id=1, replica_groups=mesh['gx'=8,'gy'=2,'gz'=2] {'gx','gy','gz'}, dimensions={0} | all-to-all | bytes 32768 | tf_op jit(solution)/shard_map/all_to_all | solution.py:383
  58.8 1.5 %finish.1 = (f32[8,8,128]{2,1,0:T(8,128)}, f32[1,128]{1,0:T(1,128)}) custom-call(f32[32,1,128]{2,1,0:T(1,128)} %all_to_all.5.got, f32[8,8,128]{2,1,0:T(8,128)} %get-tuple-element.27.sens), custom_call_target="tpu_custom_call" | custom-call | tf_op jit(solution)/shard_map/finish/pallas_call | solution.py:350
  60.4 1.3 %fusion = (f32[1,1]{1,0:T(1,128)}, f32[1,1]{1,0:T(1,128)}) fusion(f32[1,128]{1,0:T(1,128)} %get-tuple-element.29), kind=kLoop, calls=%fused_computation | loop fusion | bytes 16 | tf_op jit(solution)/shard_map/slice | solution.py:385
  (18 shorter events, 3.5 us)
Async XLA Ops:
  2.3 1.5 %collective-permute-start = (f32[5,8,128]{2,1,0:T(8,128)}, f32[5,8,128]{2,1,0:T(8,128)S(1)}, u32[]{:S(2)}, u32[]{:S(2)}) collective-permute-start(f32[5,8,128]{2,1,0:T(8,128)} %pack_y.1), channel_id=1, source_target_pairs={{0,2},{2,0},{1,3},{3,1},{4,6},{6,4},{5,7},{7,5},{8,10},{10,8},{9,1... | collective-permute-start | bytes 61448 | tf_op jit(solution)/shard_map/ppermute | solution.py:178
  3.9 0.6 copy-start.1
  6.3 4.6 %collective-permute-start.1 = (f32[1,8,128]{2,1,0:T(8,128)}, f32[1,8,128]{2,1,0:T(8,128)S(1)}, u32[]{:S(2)}, u32[]{:S(2)}) collective-permute-start(f32[1,8,128]{2,1,0:T(8,128)} %pack_z.2), channel_id=1, source_target_pairs={{0,1},{1,0},{2,3},{3,2},{4,5},{5,4},{6,7},{7,6},{8,9},{9,8},{10,11... | collective-permute-start | bytes 12296 | tf_op jit(solution)/shard_map/ppermute | solution.py:178
  10.9 0.6 copy-start.7
  13.3 4.0 %collective-permute-start.2 = (f32[5,8,128]{2,1,0:T(8,128)}, f32[5,8,128]{2,1,0:T(8,128)S(1)}, u32[]{:S(2)}, u32[]{:S(2)}) collective-permute-start(f32[5,8,128]{2,1,0:T(8,128)} %get-tuple-element.17), channel_id=1, source_target_pairs={{0,4},{4,0},{8,12},{12,8},{16,20},{20,16},{24,28},{28,24},{1,5},{5... | collective-permute-start | bytes 61448 | tf_op jit(solution)/shard_map/ppermute | solution.py:178
  15.4 2.0 %collective-permute-start.3 = (f32[5,8,128]{2,1,0:T(8,128)}, f32[5,8,128]{2,1,0:T(8,128)S(1)}, u32[]{:S(2)}, u32[]{:S(2)}) collective-permute-start(f32[5,8,128]{2,1,0:T(8,128)} %get-tuple-element.18), channel_id=1, source_target_pairs={{0,0},{4,8},{8,4},{12,16},{16,12},{20,24},{24,20},{28,28},{1,1},{5... | collective-permute-start | bytes 61448 | tf_op jit(solution)/shard_map/ppermute | solution.py:178
  17.3 0.6 copy-start.3
  17.9 0.6 copy-start.5
  21.5 1.4 %collective-permute-start.4 = (f32[5,8,128]{2,1,0:T(8,128)}, f32[5,8,128]{2,1,0:T(8,128)S(1)}, u32[]{:S(2)}, u32[]{:S(2)}) collective-permute-start(f32[5,8,128]{2,1,0:T(8,128)} %get-tuple-element.20), channel_id=1, source_target_pairs={{0,2},{2,0},{1,3},{3,1},{4,6},{6,4},{5,7},{7,5},{8,10},{10,8},{9,1... | collective-permute-start | bytes 61448 | tf_op jit(solution)/shard_map/ppermute | solution.py:178
  22.9 0.6 copy-start
  25.4 3.8 %collective-permute-start.5 = (f32[1,8,128]{2,1,0:T(8,128)}, f32[1,8,128]{2,1,0:T(8,128)S(1)}, u32[]{:S(2)}, u32[]{:S(2)}) collective-permute-start(f32[1,8,128]{2,1,0:T(8,128)} %pack_z.3), channel_id=1, source_target_pairs={{0,1},{1,0},{2,3},{3,2},{4,5},{5,4},{6,7},{7,6},{8,9},{9,8},{10,11... | collective-permute-start | bytes 12296 | tf_op jit(solution)/shard_map/ppermute | solution.py:178
  29.2 0.6 copy-start.6
  31.5 6.3 %collective-permute-start.6 = (f32[5,8,128]{2,1,0:T(8,128)}, f32[5,8,128]{2,1,0:T(8,128)S(1)}, u32[]{:S(2)}, u32[]{:S(2)}) collective-permute-start(f32[5,8,128]{2,1,0:T(8,128)} %get-tuple-element.21), channel_id=1, source_target_pairs={{0,4},{4,0},{8,12},{12,8},{16,20},{20,16},{24,28},{28,24},{1,5},{5... | collective-permute-start | bytes 61448 | tf_op jit(solution)/shard_map/ppermute | solution.py:178
  35.9 2.0 %collective-permute-start.7 = (f32[5,8,128]{2,1,0:T(8,128)}, f32[5,8,128]{2,1,0:T(8,128)S(1)}, u32[]{:S(2)}, u32[]{:S(2)}) collective-permute-start(f32[5,8,128]{2,1,0:T(8,128)} %get-tuple-element.22), channel_id=1, source_target_pairs={{0,0},{4,8},{8,4},{12,16},{16,12},{20,24},{24,20},{28,28},{1,1},{5... | collective-permute-start | bytes 61448 | tf_op jit(solution)/shard_map/ppermute | solution.py:178
  37.9 0.6 copy-start.2
  37.9 0.6 copy-start.4

commit v3 on v2

--- a/solution.py
+++ b/solution.py
@@ -19,6 +19,9 @@
 inflow_speed = 0.08
 ups = [[i for i in range(19) if lattice[i][d] == 1] for d in range(3)]
 downs = [[i for i in range(19) if lattice[i][d] == -1] for d in range(3)]
+flats = [[i for i in range(19) if lattice[i][d] == 0] for d in range(3)]
+z_low = downs[2]
+z_high = [lattice.index((x, y, 1)) for x, y, _ in (lattice[i] for i in z_low)]
 
 
 def relax_factors():
@@ -43,7 +46,7 @@
 factor = relax_factors()
 
 
-def flow_of(d, g):
+def flow_of(d, g, solid, kind):
     rho = d[0]
     for i in range(1, 19):
         rho = rho + d[i]
@@ -55,17 +58,20 @@
     iden = 1.0 / ((convexity + mixed) + (1.0 - mixed) * g)
     irho = 1.0 / rho
     damp = (convexity + g) * iden
-    slope = (mixed * (1.0 + convexity)) * (iden * iden)
     beta = damp * irho
-    return rho, irho, jx * beta, jy * beta, jz * beta, beta, (jx * irho, jy * irho, jz * irho), slope
-
-
-def local_adjoint(p, flow, solid, kind, wt):
-    rho, irho, ux, uy, uz, beta = flow[:6]
-    is_solid = solid == 1
-    fluid = solid == 0
-    inlet = kind == 1
-    outlet = kind == 2
+    ux, uy, uz = jx * beta, jy * beta, jz * beta
+    code = jnp.where(solid == 1, -2.0, jnp.where(kind == 1, -1.0, jnp.where(kind == 2, irho, 0.0)))
+    slope = jnp.where(solid == 1, 0.0, (mixed * (1.0 + convexity)) * rho * iden / (convexity + g))
+    energy = jnp.where(solid == 0, rho * (ux * ux + uy * uy + uz * uz), 0.0)
+    return ux, uy, uz, damp, code, slope, energy
+
+
+def local_adjoint(p, flow, wt):
+    ux, uy, uz, damp, code = flow[:5]
+    is_solid = code < -1.5
+    inlet = jnp.logical_and(code < -0.5, code > -1.5)
+    outlet = code > 0.0
+    inside = code == 0.0
     pairs = (1, 3, 5, 7, 9, 11, 13, 15, 17)
     he = {k: 0.5 * (p[k] + p[k + 1]) for k in pairs}
     ho = {k: 0.5 * (p[k] - p[k + 1]) for k in pairs}
@@ -135,17 +141,18 @@
         (base / 3.0) * p[0] + (n * full) * he[1] + (n * 3.0 * us) * ho[1] + (n * base) * (he[3] + he[5])
         + (d * full) * (xy + xz) + (d * 3.0 * us) * (xa + xb) + (d * base) * yz
     )
-    scale = jnp.where(inlet, 0.0, jnp.where(outlet, 1.0, rho))
-    kin = wt * rho
-    lx = scale * (3.0 * s1x + 9.0 * vx - 3.0 * ux * s0) + kin * ux
-    ly = scale * (3.0 * s1y + 9.0 * vy - 3.0 * uy * s0) + kin * uy
-    lz = scale * (3.0 * s1z + 9.0 * vz - 3.0 * uz * s0) + kin * uz
-    r = jnp.where(inlet, q_in, jnp.where(outlet, 0.0, d_rho)) + 0.5 * wt * usq
-    r = r - (lx * ux + ly * uy + lz * uz) * irho
+    lx = 3.0 * s1x + 9.0 * vx - 3.0 * ux * s0
+    ly = 3.0 * s1y + 9.0 * vy - 3.0 * uy * s0
+    lz = 3.0 * s1z + 9.0 * vz - 3.0 * uz * s0
+    scale = jnp.where(inside, 1.0, jnp.where(outlet, code, 0.0))
+    pull = (lx * ux + ly * uy + lz * uz) * scale
+    sens = pull + wt * usq
+    r = jnp.where(inside, d_rho, jnp.where(inlet, q_in, 0.0)) - (pull + (0.5 * wt) * usq)
     r = jnp.where(is_solid, 0.0, r)
-    bs = jnp.where(is_solid, 0.0, beta)
-    gx, gy, gz = lx * bs, ly * bs, lz * bs
-    inside = jnp.logical_not(is_solid | inlet | outlet)
+    ds = jnp.where(is_solid, 0.0, damp)
+    dl = ds * scale
+    dw = ds * wt
+    gx, gy, gz = lx * dl + ux * dw, ly * dl + uy * dw, lz * dl + uz * dw
     on = jnp.where(inside, 1.0, 0.0)
     keep = jnp.where(is_solid, 1.0, on)
     flip = jnp.where(is_solid, -1.0, on)
@@ -157,8 +164,7 @@
         odd = flux[k] + (flip * ho[k] - on * ro[k])
         out[k] = even + odd
         out[k + 1] = even - odd
-    cost = jnp.where(fluid, 0.5 * kin * usq, 0.0)
-    return out, (lx, ly, lz), cost
+    return out, sens
 
 
 def swap_pairs(size, odd):
@@ -231,158 +237,335 @@
     return jnp.where(lane == at, column, roll(tile, -cz, 1))
 
 
-def y_rows(links, refs):
-    return [links[1].above(refs, k) for k in range(5)], [links[1].below(refs, k) for k in range(5)]
-
-
-def pack_y(links, a, out):
+def z_column(i, x, messages, lane):
+    above, below = messages
+    if lattice[i][2] == 1:
+        return roll(above[0], 127 - (ups[2].index(i) * 8 + x), 1)
+    return roll(below[0], -(downs[2].index(i) * 8 + x), 1)
+
+
+class Pull:
+    def __init__(self, links, a, ys, zs=None):
+        self.sub, self.lane = iotas()
+        self.a = a
+        self.y_above = [links[1].above(ys, k) for k in range(5)]
+        self.y_below = [links[1].below(ys, k) for k in range(5)]
+        if zs is not None:
+            self.z_above = [links[2].above(zs, k) for k in range(2)]
+            self.z_below = [links[2].below(zs, k) for k in range(2)]
+
+    def along_y(self, i, x):
+        return shift_y(self.a[i, x], i, x, self.y_above, self.y_below, self.sub)
+
+    def tile(self, i, x):
+        return shift_z(self.along_y(i, x), i, x, self.z_above[0], self.z_below[0], self.lane)
+
+
+def place(tiles, q, base):
+    return roll(tiles[q // 16], base - (q % 16) * 8, 1)
+
+
+def weight_at(position, whole_x):
+    return 1.0 + 2.0 * position.astype(jnp.float32) / (whole_x - 1)
+
+
+def pack_y_kernel(links, a, *out):
     for k in range(5):
-        up = a[downs[1][k], :, 7, :]
-        down = a[ups[1][k], :, 0, :]
-        links[1].emit(out, k, up, down)
-
-
-def pack_z(links, a, ys, out):
+        links[1].emit(out, k, a[downs[1][k], :, 7, :], a[ups[1][k], :, 0, :])
+
+
+def flow_kernel(t, states, g, solid, kind, after, *refs):
+    whole_x = t[1]
+    t = t[0]
+    if t == 0:
+        cost_in, *refs = refs
+    flow, cost, held, done = refs
+    copy = pltpu.make_async_copy(states.at[t], held, done)
+    copy.start()
+    copy.wait()
+    start = lax.axis_index("gx") * 8
+    total = jnp.zeros((8, 128), jnp.float32) if t else cost_in[...]
+    for x in range(8):
+        values = flow_of([held[i, x] for i in range(19)], g[x], solid[x], kind[x])
+        for k in range(6):
+            flow[k, x] = values[k]
+        total = total + (0.5 * weight_at(start + x, whole_x)) * values[6]
+    cost[...] = total
+
+
+def pack_z_kernel(links, a, flow, *refs):
+    n, m = links[1].count, links[2].count
+    ys, out, own = refs[:n], refs[n : n + m], refs[n + m]
+    pull = Pull(links, a, ys)
+    lane = pull.lane
+    both = []
+    for near, far, moving in ((127, 126, downs[2]), (0, 1, ups[2])):
+        tiles = [jnp.zeros((8, 128), jnp.float32)] * 2
+        for q in range(24):
+            for x in range(8):
+                at = (q % 16) * 8 + x
+                if q < 10:
+                    tile, column = pull.along_y(moving[q % 5], x), near if q < 5 else far
+                else:
+                    tile, column = pull.along_y(flats[2][q - 10], x) if q < 19 else flow[q - 19, x], near
+                tiles[q // 16] = jnp.where(lane == at, roll(tile, at - column, 1), tiles[q // 16])
+        both.append(tiles)
+    for k in range(2):
+        own[k] = both[k][0]
+        links[2].emit(out, k, both[0][k], both[1][k])
+
+
+def pack_x_kernel(links, whole_x, a, flow, own, *refs):
+    n, m, c = links[1].count, links[2].count, links[0].count
+    ys, zs, out, side = refs[:n], refs[n : n + m], refs[n + m : n + m + c], refs[n + m + c]
+    pull = Pull(links, a, ys, zs)
+    lane = pull.lane
+    half = lane & 63
+    edge = []
+    for i in range(19):
+        cz = lattice[i][2]
+        if cz == 0:
+            k = flats[2].index(i)
+            low, high = place(pull.z_below, 10 + k, 1), place(pull.z_above, 10 + k, 65)
+        elif cz == 1:
+            k = ups[2].index(i)
+            low, high = place([own[1]], k, 1), place(pull.z_above, 5 + k, 65)
+        else:
+            k = downs[2].index(i)
+            low, high = place(pull.z_below, 5 + k, 1), place([own[0]], k, 65)
+        edge.append(jnp.where(lane < 64, low, high))
+    for k in range(5):
+        low, high = place(pull.z_below, 19 + k, 1), place(pull.z_above, 19 + k, 65)
+        edge.append(jnp.where(lane < 64, low, high))
+    for k in range(24):
+        side[k] = edge[k]
+    start = lax.axis_index("gx") * 8
+    both = []
+    for near, far, moving in ((7, 6, downs[0]), (0, 1, ups[0])):
+        tiles = [pull.tile(i, near) for i in moving]
+        p = [jnp.zeros((8, 128), jnp.float32)] * 19
+        for i in moving:
+            p[i] = pull.tile(i, far)
+        for i in flats[0]:
+            p[i] = pull.tile(i, near)
+        part, _ = local_adjoint(p, [flow[k, near] for k in range(5)], weight_at(start + near, whole_x))
+        tiles += [part[i] for i in moving] + [flow[k, near] for k in range(5)]
+        columns = jnp.zeros((8, 128), jnp.float32)
+        sources = [(edge[i], near) for i in moving] + [(edge[i], far) for i in moving]
+        sources += [(edge[i], near) for i in flats[0]] + [(edge[19 + k], near) for k in range(5)]
+        for q, (tile, x) in enumerate(sources):
+            columns = jnp.where(half == q, roll(tile, q - (x + 1), 1), columns)
+        both.append(tiles + [columns])
+    for k in range(16):
+        links[0].emit(out, k, both[0][k], both[1][k])
+
+
+def step_1_kernel(links, whole_x, a, flow, side, *refs):
+    n, m, c = links[1].count, links[2].count, links[0].count
+    refs = list(refs)
+    take = lambda k: [refs.pop(0) for _ in range(k)]
+    ys, zs, xs = take(n), take(m), take(c)
+    new, beside_x, beside_z, sens = take(4)
+    out_y = refs
+    pull = Pull(links, a, ys, zs)
+    sub, lane = pull.sub, pull.lane
+    half = lane & 63
+    start = lax.axis_index("gx") * 8
+    above = [links[0].above(xs, k) for k in range(16)]
+    below = [links[0].below(xs, k) for k in range(16)]
+    first_x, last_x = links[0].ends()
+    first_z, last_z = links[2].ends()
+    for x in range(8):
+        p = []
+        for i in range(19):
+            to = x + lattice[i][0]
+            if to < 0:
+                p.append(below[downs[0].index(i)])
+            elif to > 7:
+                p.append(above[ups[0].index(i)])
+            else:
+                p.append(pull.tile(i, to))
+        out, s = local_adjoint(p, [flow[k, x] for k in range(5)], weight_at(start + x, whole_x))
+        for i in range(19):
+            new[i, x] = out[i]
+        sens[x] = s * flow[5, x]
+    for base, near, mine, moving, got, absent in (
+        (0, 0, ups[0], downs[0], below, first_x), (5, 7, downs[0], ups[0], above, last_x)
+    ):
+        p = [jnp.zeros((8, 128), jnp.float32)] * 19
+        for i in mine:
+            p[i] = pull.tile(i, near)
+        out, _ = local_adjoint(p, got[10:15], 0.0)
+        for k, i in enumerate(moving):
+            beside_x[base + k] = jnp.where(absent, 0.0, out[i] + got[5 + k])
+    def at(tile, lane_to, q):
+        return roll(tile, lane_to - q, 1)
+
+    low, high = below[15], above[15]
+    p = []
+    for i in range(19):
+        cx = lattice[i][0]
+        tile = side[i]
+        if cx == 0:
+            k = flats[0].index(i)
+            tile = jnp.where(half == 0, at(low, 0, 10 + k), jnp.where(half == 9, at(high, 9, 10 + k), tile))
+        elif cx == -1:
+            k = downs[0].index(i)
+            tile = jnp.where(half == 0, at(low, 0, 5 + k), jnp.where(half == 1, at(low, 1, k), roll(tile, 1, 1)))
+        else:
+            k = ups[0].index(i)
+            tile = jnp.where(half == 9, at(high, 9, 5 + k), jnp.where(half == 8, at(high, 8, k), roll(tile, -1, 1)))
+        p.append(tile)
+    near = [
+        jnp.where(half == 0, at(low, 0, 19 + k), jnp.where(half == 9, at(high, 9, 19 + k), side[19 + k]))
+        for k in range(5)
+    ]
+    used = half < 10
+    p = [jnp.where(used, v, 0.0) for v in p]
+    near = [jnp.where(used, v, 0.0) for v in near]
+    out, _ = local_adjoint(p, near, weight_at(start - 1 + half, whole_x))
+    here = jnp.where(lane < 64, jnp.where(first_z, 0.0, 1.0), jnp.where(last_z, 0.0, 1.0))
+    here = jnp.where(half == 0, jnp.where(first_x, 0.0, here), jnp.where(half == 9, jnp.where(last_x, 0.0, here), here))
+    here = jnp.where(used, here, 0.0)
+    for k in range(5):
+        beside_z[k] = here * jnp.where(lane < 64, out[z_low[k]], out[z_high[k]])
+    for k in range(5):
+        links[1].emit(out_y, k, new[downs[1][k], :, 7, :], new[ups[1][k], :, 0, :])
+    both = []
+    for cy, row in ((-1, 7), (1, 0)):
+        left = beside_x[downs[0].index(lattice.index((-1, cy, 0)))][row : row + 1, :]
+        right = beside_x[5 + ups[0].index(lattice.index((1, cy, 0)))][row : row + 1, :]
+        edge = beside_z[z_low.index(lattice.index((0, cy, -1)))][row : row + 1, :]
+        both.append(jnp.where(sub == 0, left, jnp.where(sub == 1, right, edge)))
+    links[1].emit(out_y, 5, *both)
+
+
+def step_0_kernel(links, whole_x, a, beside_x, beside_z, flow, sens_in, cost_in, *refs):
+    n = links[1].count
+    ys = refs[:n]
+    new, sens, sums = refs[n:]
     sub, lane = iotas()
-    y_above, y_below = y_rows(links, ys)
-    even = lax.axis_index("gz") % 2 == 0
-    up, down = jnp.zeros((8, 128), jnp.float32), jnp.zeros((8, 128), jnp.float32)
+    y_above = [links[1].above(ys, k) for k in range(6)]
+    y_below = [links[1].below(ys, k) for k in range(6)]
+    start = lax.axis_index("gx") * 8
+
+    def moved_y(tile, i, row):
+        cy = lattice[i][1]
+        if cy == 0:
+            return tile
+        row = jnp.broadcast_to((y_above if cy == 1 else y_below)[5][row : row + 1, :], (8, 128))
+        return jnp.where(sub == (7 if cy == 1 else 0), row, roll(tile, -cy, 0))
+
+    columns = {}
     for k in range(5):
-        for x in range(8):
-            at = k * 8 + x
-            i, j = downs[2][k], ups[2][k]
-            tile = roll(shift_y(a[i, x], i, x, y_above, y_below, sub), at - 127, 1)
-            up = jnp.where(lane == at, tile, up)
-            tile = roll(shift_y(a[j, x], j, x, y_above, y_below, sub), at, 1)
-            down = jnp.where(lane == at, tile, down)
-    links[2].emit(out, 0, up, down)
-
-
-def pack_x(links, a, ys, zs, out):
-    sub, lane = iotas()
-    y_above, y_below = y_rows(links, ys)
-    z_above, z_below = links[2].above(zs, 0), links[2].below(zs, 0)
-    for k in range(5):
-        both = []
-        for i, x in ((downs[0][k], 7), (ups[0][k], 0)):
-            tile = shift_y(a[i, x], i, x, y_above, y_below, sub)
-            both.append(shift_z(tile, i, x, z_above, z_below, lane))
-        links[0].emit(out, k, *both)
-
-
-def pack_z_kernel(links, a, *refs):
-    n = links[1].count
-    pack_z(links, a, refs[:n], refs[n:])
-
-
-def pack_x_kernel(links, a, *refs):
-    n, m = links[1].count, links[2].count
-    pack_x(links, a, refs[:n], refs[n : n + m], refs[n + m :])
-
-
-def pack_y_kernel(links, a, *refs):
-    pack_y(links, a, refs)
-
-
-def step_kernel(links, whole_x, last, a, states, g, solid, kind, *refs):
-    counts = [links[1].count, links[2].count, links[0].count]
-    refs = list(refs)
-    take = lambda n: [refs.pop(0) for _ in range(n)]
-    ys, zs, xs = (take(c) for c in counts)
-    if last:
-        sens_in, cost_in = take(2)
-    new, sens, cost = take(3)
-    sub, lane = iotas()
-    y_above, y_below = y_rows(links, ys)
-    z_above, z_below = links[2].above(zs, 0), links[2].below(zs, 0)
-    start = lax.axis_index("gx") * 8
-    total = jnp.zeros((8, 128), jnp.float32)
+        both = moved_y(beside_z[k], z_low[k], 2)
+        columns[z_low[k]] = columns[z_high[k]] = both
+
     squares = jnp.zeros((8, 128), jnp.float32)
     for x in range(8):
         p = []
         for i in range(19):
-            cx = lattice[i][0]
-            if not 0 <= x + cx < 8:
-                k = (ups if cx == 1 else downs)[0].index(i)
-                p.append((links[0].above if cx == 1 else links[0].below)(xs, k))
-                continue
-            tile = shift_y(a[i, x + cx], i, x + cx, y_above, y_below, sub)
-            p.append(shift_z(tile, i, x + cx, z_above, z_below, lane))
-        d = [states[0 if last else 1, i, x] for i in range(19)]
-        flow = flow_of(d, g[x])
-        wt = 1.0 + 2.0 * (start + x).astype(jnp.float32) / (whole_x - 1)
-        out, force, k_cell = local_adjoint(p, flow, solid[x], kind[x], wt)
+            cx, cy, cz = lattice[i]
+            to = x + cx
+            if to < 0:
+                tile = moved_y(beside_x[downs[0].index(i)], i, 0)
+            elif to > 7:
+                tile = moved_y(beside_x[5 + ups[0].index(i)], i, 1)
+            else:
+                tile = shift_y(a[i, to], i, to, y_above, y_below, sub)
+            if cz:
+                at = 127 if cz == 1 else 0
+                held = (65 if cz == 1 else 1) + to
+                tile = jnp.where(lane == at, roll(columns[i], at - held, 1), roll(tile, -cz, 1))
+            p.append(tile)
+        out, s = local_adjoint(p, [flow[k, x] for k in range(5)], weight_at(start + x, whole_x))
         for i in range(19):
             new[i, x] = out[i]
-        v = flow[6]
-        s = (force[0] * v[0] + force[1] * v[1] + force[2] * v[2]) * flow[7]
-        s = jnp.where(solid[x] == 1, 0.0, s)
-        total = total + k_cell
-        if last:
-            s = s + sens_in[x]
-            squares = squares + s * s
+        s = s * flow[5, x] + sens_in[x]
+        squares = squares + s * s
         sens[x] = s
-    if last:
-        total = jnp.sum(total + cost_in[...], axis=0, keepdims=True)
-        squares = jnp.sum(squares, axis=0, keepdims=True)
-        both = jnp.where(lane[:1] < 64, jnp.sum(total), jnp.sum(squares))
-        cost[...] = jnp.broadcast_to(both[None], cost.shape)
-    else:
-        cost[...] = total
-        pack_y(links, new, refs)
-
-
-def finish_kernel(cells, got, sens, out, scalars):
+    total = jnp.sum(jnp.sum(cost_in[...], axis=0, keepdims=True))
+    both = jnp.where(lane[:1] < 64, total, jnp.sum(jnp.sum(squares, axis=0, keepdims=True)))
+    sums[...] = jnp.broadcast_to(both[None], sums.shape)
+
+
+def finish_kernel(cells, got, sens, out, objective, sens_rms):
     sums = jnp.sum(got[...], axis=0)
     cost = jnp.sum(sums[:, :1])
     square = jnp.sum(sums[:, 64:65])
-    lane = lax.broadcasted_iota(jnp.int32, (1, 128), 1)
     rms = jnp.sqrt(jnp.broadcast_to(square / cells, (1, 128)) + 1e-06)
     out[...] = sens[...] / jnp.broadcast_to(rms[None], sens.shape)
-    scalars[...] = jnp.where(lane < 64, jnp.broadcast_to(cost / cells, (1, 128)), rms)
+    objective[0, 0] = cost / cells
+    sens_rms[0, 0] = jnp.max(rms)
 
 
 vmem = pl.BlockSpec(memory_space=pltpu.VMEM)
-
-
-def call(kernel, outs, *args, name):
-    shapes = tuple(jax.ShapeDtypeStruct(s, jnp.float32) for s in outs)
+smem = pl.BlockSpec(memory_space=pltpu.SMEM)
+hbm = pl.BlockSpec(memory_space=pl.ANY)
+
+
+def call(kernel, outs, *args, name, plain=(), scalar=(), unplaced=(), scratch=(), cost=None):
+    shapes = tuple(
+        jax.ShapeDtypeStruct(s, jnp.float32) if k in plain or k in scalar else pltpu.VMEM(s, jnp.float32)
+        for k, s in enumerate(outs)
+    )
+    args = [x if k in unplaced else pltpu.with_memory_space_constraint(x, pltpu.VMEM) for k, x in enumerate(args)]
     return pl.pallas_call(
-        kernel, out_shape=shapes, in_specs=[vmem] * len(args), out_specs=tuple([vmem] * len(outs)), name=name
+        kernel,
+        out_shape=shapes,
+        in_specs=[hbm if k in unplaced else vmem for k in range(len(args))],
+        out_specs=tuple(smem if k in scalar else vmem for k in range(len(outs))),
+        scratch_shapes=scratch,
+        cost_estimate=cost,
+        name=name,
     )(*args)
-
-
-def pull_messages(links, a, y_messages):
-    ys = links[1].swap(y_messages)
-    zs = call(partial(pack_z_kernel, links), [(1, 8, 128)] * links[2].count, a, *ys, name="pack_z")
-    zs = links[2].swap(zs)
-    xs = call(partial(pack_x_kernel, links), [(5, 8, 128)] * links[0].count, a, *ys, *zs, name="pack_x")
-    xs = links[0].swap(xs)
-    return (*ys, *zs, *xs)
 
 
 def body(sizes, a, states, design, solid, kind):
     links = [Link(axis, sizes[axis]) for axis in axes]
     devices = sizes["gx"] * sizes["gy"] * sizes["gz"]
-    assert design.shape == (8, 8, 128)
+    block = design.shape
+    assert block == (8, 8, 128)
     cells = devices * design.size
     whole_x = sizes["gx"] * 8
-    field = a.shape
-    y_shapes = [(5, 8, 128)] * links[1].count
-    ys = call(partial(pack_y_kernel, links), y_shapes, a, name="pack_y")
-    messages = pull_messages(links, a, ys)
-    a, sens, cost, *ys = call(
-        partial(step_kernel, links, whole_x, False), [field, design.shape, (8, 128), *y_shapes],
-        a, states, design, solid, kind, *messages, name="step_1",
-    )
-    messages = pull_messages(links, a, ys)
+    tile = (8, 128)
+    held = [pltpu.VMEM(a.shape, jnp.float32), pltpu.SemaphoreType.DMA]
+    count = pl.CostEstimate(flops=4 * 10**6, bytes_accessed=10**6, transcendentals=0)
+
+    ys = call(partial(pack_y_kernel, links), [(5, *tile)] * links[1].count, a, name="pack_y")
+    flow, cost = call(
+        partial(flow_kernel, (1, whole_x)), [(6, *block), tile], states, design, solid, kind, ys[0],
+        name="flow_1", unplaced=(0,), scratch=held, cost=count,
+    )
+    ys = links[1].swap(ys)
+    *zs, own = call(
+        partial(pack_z_kernel, links), [(2, *tile)] * (links[2].count + 1), a, flow, *ys, name="pack_z"
+    )
+    zs = links[2].swap(zs)
+    *xs, side = call(
+        partial(pack_x_kernel, links, whole_x), [(16, *tile)] * links[0].count + [(24, *tile)],
+        a, flow, own, *ys, *zs, name="pack_x",
+    )
+    flow_0, cost = call(
+        partial(flow_kernel, (0, whole_x)), [(6, *block), tile], states, design, solid, kind, xs[-1], cost,
+        name="flow_0", unplaced=(0,), scratch=held, cost=count,
+    )
+    xs = links[0].swap(xs)
+    a, beside_x, beside_z, sens, *ys = call(
+        partial(step_1_kernel, links, whole_x),
+        [a.shape, (10, *tile), (5, *tile), block] + [(6, *tile)] * links[1].count,
+        a, flow, side, *ys, *zs, *xs, name="step_1",
+    )
+    ys = links[1].swap(ys)
     a, sens, sums = call(
-        partial(step_kernel, links, whole_x, True), [field, design.shape, (devices, 1, 128)],
-        a, states, design, solid, kind, *messages, sens, cost, name="step_0",
+        partial(step_0_kernel, links, whole_x), [a.shape, block, (devices, 1, 128)],
+        a, beside_x, beside_z, flow_0, sens, cost, *ys, name="step_0", plain=(0,),
     )
     got = lax.all_to_all(sums, axes, 0, 0)
-    sens, scalars = call(partial(finish_kernel, cells), [design.shape, (1, 128)], got, sens, name="finish")
-    return a, sens, scalars[0, 0], scalars[0, 64]
+    sens, objective, sens_rms = call(
+        partial(finish_kernel, cells), [block, (1, 1), (1, 1)], got, sens, name="finish", plain=(0,), scalar=(1, 2)
+    )
+    return a, sens, objective.reshape(()), sens_rms.reshape(())
 
 
 def solution(mesh):

time: 62.2 us -> 36.7 us (0.59)
  Pallas kernels: 16.5 us -> 6.11 us
  starting transfers between devices: 14.4 us -> 6.02 us
  waiting for transfers between devices: 7.26 us -> 3.22 us
  local copies, waits for them, and re-layouts: 5.46 us -> 3.36 us
    pallas_call x8, Pallas kernels: 16.5 us -> 6.11 us  [call(): pl.pallas_call(kernel, out_shape=shapes, in_specs=[hbm if k in unplaced e...]
    ppermute x8 -> x5, starting transfers between devices: 14.4 us -> 6.02 us  [swap(): lax.ppermute(m, self.axis, swap_pairs(self.size, k))]
    ppermute x8 -> x5, waiting for transfers between devices: 7.26 us -> 3.22 us  [swap(): lax.ppermute(m, self.axis, swap_pairs(self.size, k))]
    slice x1 -> x0, local copies, waits for them, and re-layouts: 1.27 us -> none  [body(): return (a, sens, scalars[0, 0], scalars[0, 64])]
    unnamed x16, local copies, waits for them, and re-layouts: 4.19 us -> 3.36 us
  transfers between devices with their start and end apart: 8 -> 5, of which waited for: 6 -> 2; matrix products, arithmetic and copies ran while one was open for 0% -> 0% of each run, Pallas kernels for 0% -> 6%
where the time goes in v3:
time: 36.7 us; the launch traced here: 36.3 us
  blocking collectives  16.8 us (46%)
  Pallas kernels  6.11 us (17%)
  starting transfers between devices  6.02 us (16%)
  local copies, waits for them, and re-layouts  3.36 us (9%)
  waiting for transfers between devices  3.22 us (9%)
  between operations  0.78 us (2%)
    all_to_all x1, blocking collectives, body(): got = lax.all_to_all(sums, axes, 0, 0)  16.8 us
    pallas_call x8, Pallas kernels, call(): pl.pallas_call(kernel, out_shape=shapes, in_specs=[hbm if k in unplaced e...  6.11 us
    ppermute x5, starting transfers between devices, swap(): lax.ppermute(m, self.axis, swap_pairs(self.size, k))  6.02 us
    unnamed x16, local copies, waits for them, and re-layouts  3.36 us
    ppermute x5, waiting for transfers between devices, swap(): lax.ppermute(m, self.axis, swap_pairs(self.size, k))  3.22 us
  transfers between devices with their start and end apart: 5, of which 2 were waited for; matrix products, arithmetic and copies ran while one was open for 0% of the time, Pallas kernels for 6%

profile of v3, /device:TPU:0, one launch (start us, length us, event | category | flops | bytes accessed | tf_op | source)
XLA Modules:
  0.0 36.3 jit_solution(16651089991727615081)
XLA Ops:
  0.6 1.1 %copy-done = f32[19,8,8,128]{3,2,1,0:T(8,128)S(1)} copy-done((f32[19,8,8,128]{3,2,1,0:T(8,128)S(1)}, f32[19,8,8,128]{3,2,1,0:T(8,128)}, u32[]{:S(2)}) %copy-start) | copy-done | bytes 622616
  1.7 0.6 %collective-permute-start = (f32[5,8,128]{2,1,0:T(8,128)S(1)}, f32[5,8,128]{2,1,0:T(8,128)S(1)}, u32[]{:S(2)}, u32[]{:S(2)}) collective-permute-start(f32[5,8,128]{2,1,0:T(8,128)S(1)} %pack_y.1.after), channel_id=1, source_target_pairs={{0,2},{2,0},{1,3},{3,1},{4,6},{6,4},{5,7},{7,5},{8,10},{10,8},{9,1... | collective-permute-start | bytes 61448 | tf_op jit(solution)/shard_map/ppermute | solution.py:184
  2.3 0.8 %copy-done.2 = f32[8,8,128]{2,1,0:T(8,128)S(1)} copy-done((f32[8,8,128]{2,1,0:T(8,128)S(1)}, f32[8,8,128]{2,1,0:T(8,128)}, u32[]{:S(2)}) %copy-start.2) | copy-done | bytes 32792
  3.1 0.8 %copy-done.4 = s32[8,8,128]{2,1,0:T(8,128)S(1)} copy-done((s32[8,8,128]{2,1,0:T(8,128)S(1)}, s32[8,8,128]{2,1,0:T(8,128)}, u32[]{:S(2)}) %copy-start.4) | copy-done | bytes 32792
  3.8 0.8 %copy-done.6 = s32[8,8,128]{2,1,0:T(8,128)S(1)} copy-done((s32[8,8,128]{2,1,0:T(8,128)S(1)}, s32[8,8,128]{2,1,0:T(8,128)}, u32[]{:S(2)}) %copy-start.6) | copy-done | bytes 32792
  4.6 1.2 %flow_1.1 = (f32[6,8,8,128]{3,2,1,0:T(8,128)S(1)}, f32[8,128]{1,0:T(8,128)S(1)}) custom-call(f32[2,19,8,8,128]{4,3,2,1,0:T(8,128)} %states.3, f32[8,8,128]{2,1,0:T(8,128)S(1)} %copy-done.2, s32[8,8,128]{2,1,0:T(8,128)S(1)} %copy-done.4, s32[8,8,128]{2,1,0:T(8,128)S(1)} %copy-done.6, f32[5,8,128]{2,1,0:T(8,128)S(1)} %pack_y.1.after), custom_call_target="tpu_custom_call" | custom-call | flops 4000000 | bytes 1000000 | tf_op jit(solution)/shard_map/flow_1/pallas_call | solution.py:513
  5.8 0.0 copy-start.3
  5.8 0.0 copy-start.5
  5.8 0.0 copy-start.7
  5.8 0.5 %pack_z.1 = (f32[2,8,128]{2,1,0:T(8,128)S(1)}, f32[2,8,128]{2,1,0:T(8,128)S(1)}) custom-call(f32[19,8,8,128]{3,2,1,0:T(8,128)S(1)} %copy-done.1, f32[6,8,8,128]{3,2,1,0:T(8,128)S(1)} %get-tuple-element.24.flow, f32[5,8,128]{2,1,0:T(8,128)S(1)} %collective-permute-done.refs_0_), custom_call_target="tpu_custom_call" | custom-call | tf_op jit(solution)/shard_map/pack_z/pallas_call | solution.py:513
  6.3 2.6 %collective-permute-start.1 = (f32[2,8,128]{2,1,0:T(8,128)S(1)}, f32[2,8,128]{2,1,0:T(8,128)S(1)}, u32[]{:S(2)}, u32[]{:S(2)}) collective-permute-start(f32[2,8,128]{2,1,0:T(8,128)S(1)} %get-tuple-element.26), channel_id=1, source_target_pairs={{0,1},{1,0},{2,3},{3,2},{4,5},{5,4},{6,7},{7,6},{8,9},{9,8},{10,11... | collective-permute-start | bytes 24584 | tf_op jit(solution)/shard_map/ppermute | solution.py:184
  8.9 1.6 %collective-permute-done.1.refs_1_ = f32[2,8,128]{2,1,0:T(8,128)S(1)} collective-permute-done((f32[2,8,128]{2,1,0:T(8,128)S(1)}, f32[2,8,128]{2,1,0:T(8,128)S(1)}, u32[]{:S(2)}, u32[]{:S(2)}) %collective-permute-start.1) | collective-permute-done | bytes 8224 | tf_op jit(solution)/shard_map/ppermute | solution.py:184
  10.6 0.2 pack_x.1
  10.8 2.1 %collective-permute-start.2 = (f32[16,8,128]{2,1,0:T(8,128)S(1)}, f32[16,8,128]{2,1,0:T(8,128)S(1)}, u32[]{:S(2)}, u32[]{:S(2)}) collective-permute-start(f32[16,8,128]{2,1,0:T(8,128)S(1)} %get-tuple-element.28), channel_id=1, source_target_pairs={{0,4},{4,0},{8,12},{12,8},{16,20},{20,16},{24,28},{28,24},{1,5},{5... | collective-permute-start | bytes 196616 | tf_op jit(solution)/shard_map/ppermute | solution.py:184
  12.9 0.7 %collective-permute-start.3 = (f32[16,8,128]{2,1,0:T(8,128)S(1)}, f32[16,8,128]{2,1,0:T(8,128)S(1)}, u32[]{:S(2)}, u32[]{:S(2)}) collective-permute-start(f32[16,8,128]{2,1,0:T(8,128)S(1)} %get-tuple-element.29.after), channel_id=1, source_target_pairs={{0,0},{4,8},{8,4},{12,16},{16,12},{20,24},{24,20},{28,28},{1,1},{5... | collective-permute-start | bytes 196616 | tf_op jit(solution)/shard_map/ppermute | solution.py:184
  13.6 1.6 %collective-permute-done.2.refs_2_ = f32[16,8,128]{2,1,0:T(8,128)S(1)} collective-permute-done((f32[16,8,128]{2,1,0:T(8,128)S(1)}, f32[16,8,128]{2,1,0:T(8,128)S(1)}, u32[]{:S(2)}, u32[]{:S(2)}) %collective-permute-start.2) | collective-permute-done | bytes 65568 | tf_op jit(solution)/shard_map/ppermute | solution.py:184
  15.2 0.0 collective-permute-done.3.refs_3_
  15.2 0.8 %step_1.1 = (f32[19,8,8,128]{3,2,1,0:T(8,128)S(1)}, f32[10,8,128]{2,1,0:T(8,128)S(1)}, f32[5,8,128]{2,1,0:T(8,128)S(1)}, f32[8,8,128]{2,1,0:T(8,128)S(1)}, f32[6,8,128]{2,1,0:T(8,128)S(1)}) custom-call(f32[19,8,8,128]{3,2,1,0:T(8,128)S(1)} %copy-done.1, f32[6,8,8,128]{3,2,1,0:T(8,128)S(1)} %get-tuple-element.24.flow, ...), custom_call_target="tpu_custom_call" | custom-call | tf_op jit(solution)/shard_map/step_1/pallas_call | solution.py:513
  16.0 0.1 collective-permute-start.4
  16.1 1.2 %flow_0.1 = (f32[6,8,8,128]{3,2,1,0:T(8,128)S(1)}, f32[8,128]{1,0:T(8,128)S(1)}) custom-call(f32[2,19,8,8,128]{4,3,2,1,0:T(8,128)} %states.3, f32[8,8,128]{2,1,0:T(8,128)S(1)} %copy-done.3, s32[8,8,128]{2,1,0:T(8,128)S(1)} %copy-done.5, s32[8,8,128]{2,1,0:T(8,128)S(1)} %copy-done.7, f32[16,8,128]{2,1,0:T(8,128)S(1)} %get-tuple-element.29.after, ...), custom_call_target="tpu_custom_call" | custom-call | flops 4000000 | bytes 1000000 | tf_op jit(solution)/shard_map/flow_0/pallas_call | solution.py:513
  17.3 0.0 collective-permute-done.4.refs_0_
  17.3 1.4 %step_0.1 = (f32[19,8,8,128]{3,2,1,0:T(8,128)}, f32[8,8,128]{2,1,0:T(8,128)S(1)}, f32[32,1,128]{2,1,0:T(1,128)S(1)}) custom-call(f32[19,8,8,128]{3,2,1,0:T(8,128)S(1)} %get-tuple-element.30.a, f32[10,8,128]{2,1,0:T(8,128)S(1)} %get-tuple-element.31.beside_x, f32[5,8,128]{2,1,0:T(8,128)S(1)} %get-tuple-element.32.beside_z, ...), custom_call_target="tpu_custom_call" | custom-call | tf_op jit(solution)/shard_map/step_0/pallas_call | solution.py:513
  18.7 16.8 %all_to_all.5.got = f32[32,1,128]{2,1,0:T(1,128)S(1)} all-to-all(f32[32,1,128]{2,1,0:T(1,128)S(1)} %get-tuple-element.39), channel_id=1, replica_groups=mesh['gx'=8,'gy'=2,'gz'=2] {'gx','gy','gz'}, dimensions={0} | all-to-all | bytes 32768 | tf_op jit(solution)/shard_map/all_to_all | solution.py:564
  35.5 0.8 %finish.1 = (f32[8,8,128]{2,1,0:T(8,128)}, f32[1,1]{1,0:T(1,128)}, f32[1,1]{1,0:T(1,128)}) custom-call(f32[32,1,128]{2,1,0:T(1,128)S(1)} %all_to_all.5.got, f32[8,8,128]{2,1,0:T(8,128)S(1)} %get-tuple-element.40.sens), custom_call_target="tpu_custom_call" | custom-call | tf_op jit(solution)/shard_map/finish/pallas_call | solution.py:513
  (11 shorter events, 0.0 us)
Async XLA Ops:
  0.6 1.1 %copy-start = (f32[19,8,8,128]{3,2,1,0:T(8,128)S(1)}, f32[19,8,8,128]{3,2,1,0:T(8,128)}, u32[]{:S(2)}) copy-start(f32[19,8,8,128]{3,2,1,0:T(8,128)} %a.7) | copy-start | bytes 1867780
  1.7 4.1 %copy-start.1 = (f32[19,8,8,128]{3,2,1,0:T(8,128)S(1)}, f32[19,8,8,128]{3,2,1,0:T(8,128)}, u32[]{:S(2)}) copy-start(f32[19,8,8,128]{3,2,1,0:T(8,128)} %a.7) | copy-start | bytes 1867780
  1.7 4.0 %collective-permute-start = (f32[5,8,128]{2,1,0:T(8,128)S(1)}, f32[5,8,128]{2,1,0:T(8,128)S(1)}, u32[]{:S(2)}, u32[]{:S(2)}) collective-permute-start(f32[5,8,128]{2,1,0:T(8,128)S(1)} %pack_y.1.after), channel_id=1, source_target_pairs={{0,2},{2,0},{1,3},{3,1},{4,6},{6,4},{5,7},{7,5},{8,10},{10,8},{9,1... | collective-permute-start | bytes 61448 | tf_op jit(solution)/shard_map/ppermute | solution.py:184
  2.3 0.8 %copy-start.2 = (f32[8,8,128]{2,1,0:T(8,128)S(1)}, f32[8,8,128]{2,1,0:T(8,128)}, u32[]{:S(2)}) copy-start(f32[8,8,128]{2,1,0:T(8,128)} %g.3) | copy-start | bytes 98308
  3.1 0.8 %copy-start.4 = (s32[8,8,128]{2,1,0:T(8,128)S(1)}, s32[8,8,128]{2,1,0:T(8,128)}, u32[]{:S(2)}) copy-start(s32[8,8,128]{2,1,0:T(8,128)} %solid.3) | copy-start | bytes 98308
  3.8 0.8 %copy-start.6 = (s32[8,8,128]{2,1,0:T(8,128)S(1)}, s32[8,8,128]{2,1,0:T(8,128)}, u32[]{:S(2)}) copy-start(s32[8,8,128]{2,1,0:T(8,128)} %kind.3) | copy-start | bytes 98308
  5.8 10.3 %copy-start.3 = (f32[8,8,128]{2,1,0:T(8,128)S(1)}, f32[8,8,128]{2,1,0:T(8,128)}, u32[]{:S(2)}) copy-start(f32[8,8,128]{2,1,0:T(8,128)} %g.3) | copy-start | bytes 98308
  5.8 10.3 %copy-start.5 = (s32[8,8,128]{2,1,0:T(8,128)S(1)}, s32[8,8,128]{2,1,0:T(8,128)}, u32[]{:S(2)}) copy-start(s32[8,8,128]{2,1,0:T(8,128)} %solid.3) | copy-start | bytes 98308
  5.8 10.3 %copy-start.7 = (s32[8,8,128]{2,1,0:T(8,128)S(1)}, s32[8,8,128]{2,1,0:T(8,128)}, u32[]{:S(2)}) copy-start(s32[8,8,128]{2,1,0:T(8,128)} %kind.3) | copy-start | bytes 98308
  6.3 4.3 %collective-permute-start.1 = (f32[2,8,128]{2,1,0:T(8,128)S(1)}, f32[2,8,128]{2,1,0:T(8,128)S(1)}, u32[]{:S(2)}, u32[]{:S(2)}) collective-permute-start(f32[2,8,128]{2,1,0:T(8,128)S(1)} %get-tuple-element.26), channel_id=1, source_target_pairs={{0,1},{1,0},{2,3},{3,2},{4,5},{5,4},{6,7},{7,6},{8,9},{9,8},{10,11... | collective-permute-start | bytes 24584 | tf_op jit(solution)/shard_map/ppermute | solution.py:184
  10.8 4.4 %collective-permute-start.2 = (f32[16,8,128]{2,1,0:T(8,128)S(1)}, f32[16,8,128]{2,1,0:T(8,128)S(1)}, u32[]{:S(2)}, u32[]{:S(2)}) collective-permute-start(f32[16,8,128]{2,1,0:T(8,128)S(1)} %get-tuple-element.28), channel_id=1, source_target_pairs={{0,4},{4,0},{8,12},{12,8},{16,20},{20,16},{24,28},{28,24},{1,5},{5... | collective-permute-start | bytes 196616 | tf_op jit(solution)/shard_map/ppermute | solution.py:184
  12.9 2.2 %collective-permute-start.3 = (f32[16,8,128]{2,1,0:T(8,128)S(1)}, f32[16,8,128]{2,1,0:T(8,128)S(1)}, u32[]{:S(2)}, u32[]{:S(2)}) collective-permute-start(f32[16,8,128]{2,1,0:T(8,128)S(1)} %get-tuple-element.29.after), channel_id=1, source_target_pairs={{0,0},{4,8},{8,4},{12,16},{16,12},{20,24},{24,20},{28,28},{1,1},{5... | collective-permute-start | bytes 196616 | tf_op jit(solution)/shard_map/ppermute | solution.py:184
  16.0 1.3 %collective-permute-start.4 = (f32[6,8,128]{2,1,0:T(8,128)S(1)}, f32[6,8,128]{2,1,0:T(8,128)S(1)}, u32[]{:S(2)}, u32[]{:S(2)}) collective-permute-start(f32[6,8,128]{2,1,0:T(8,128)S(1)} %get-tuple-element.37), channel_id=1, source_target_pairs={{0,2},{2,0},{1,3},{3,1},{4,6},{6,4},{5,7},{7,5},{8,10},{10,8},{9,1... | collective-permute-start | bytes 73736 | tf_op jit(solution)/shard_map/ppermute | solution.py:184

commit v4 on v3

--- a/solution.py
+++ b/solution.py
@@ -7,6 +7,7 @@
 from jax.experimental import pallas as pl
 from jax.experimental.pallas import tpu as pltpu
 from jax.sharding import PartitionSpec as P
+
 
 lattice = [
     (0, 0, 0), (1, 0, 0), (-1, 0, 0), (0, 1, 0), (0, -1, 0), (0, 0, 1), (0, 0, -1),
@@ -181,7 +182,10 @@
         self.count = 1 if size == 2 else 2
 
     def swap(self, messages):
-        return [lax.ppermute(m, self.axis, swap_pairs(self.size, k)) for k, m in enumerate(messages)]
+        got = []
+        for k, m in enumerate(messages):
+            got.append(lax.ppermute(m, self.axis, swap_pairs(self.size, k)))
+        return got
 
     def emit(self, refs, slot, up, down):
         even = lax.axis_index(self.axis) % 2 == 0
@@ -235,13 +239,6 @@
     at = 127 if cz == 1 else 0
     column = roll(z_above if cz == 1 else z_below, at - (k * 8 + x), 1)
     return jnp.where(lane == at, column, roll(tile, -cz, 1))
-
-
-def z_column(i, x, messages, lane):
-    above, below = messages
-    if lattice[i][2] == 1:
-        return roll(above[0], 127 - (ups[2].index(i) * 8 + x), 1)
-    return roll(below[0], -(downs[2].index(i) * 8 + x), 1)
 
 
 class Pull:
@@ -269,24 +266,42 @@
     return 1.0 + 2.0 * position.astype(jnp.float32) / (whole_x - 1)
 
 
-def pack_y_kernel(links, a, *out):
+def pack_y_kernel(links, a, *refs):
+    *out, rows, done = refs
+    copies = []
     for k in range(5):
-        links[1].emit(out, k, a[downs[1][k], :, 7, :], a[ups[1][k], :, 0, :])
-
-
-def flow_kernel(t, states, g, solid, kind, after, *refs):
-    whole_x = t[1]
-    t = t[0]
+        for side, (i, y) in enumerate(((downs[1][k], 7), (ups[1][k], 0))):
+            copies.append(pltpu.make_async_copy(a.at[i, :, y, :], rows.at[side, k], done.at[2 * k + side]))
+    for copy in copies:
+        copy.start()
+    for copy in copies:
+        copy.wait()
+    for k in range(5):
+        links[1].emit(out, k, rows[0, k], rows[1, k])
+
+
+def flow_kernel(t, whole_x, states, g, solid, kind, after, *refs):
     if t == 0:
         cost_in, *refs = refs
-    flow, cost, held, done = refs
-    copy = pltpu.make_async_copy(states.at[t], held, done)
-    copy.start()
-    copy.wait()
+    flow, cost, held, g_held, solid_held, kind_held, done = refs
+    copies = [
+        pltpu.make_async_copy(src, dst, done.at[k])
+        for k, (src, dst) in enumerate(((g, g_held), (solid, solid_held), (kind, kind_held)))
+    ]
+    layers = [
+        pltpu.make_async_copy(states.at[t, :, pl.ds(2 * k, 2)], held.at[:, pl.ds(2 * k, 2)], done.at[3 + k])
+        for k in range(4)
+    ]
+    for copy in copies + layers:
+        copy.start()
+    for copy in copies:
+        copy.wait()
     start = lax.axis_index("gx") * 8
     total = jnp.zeros((8, 128), jnp.float32) if t else cost_in[...]
     for x in range(8):
-        values = flow_of([held[i, x] for i in range(19)], g[x], solid[x], kind[x])
+        if x % 2 == 0:
+            layers[x // 2].wait()
+        values = flow_of([held[i, x] for i in range(19)], g_held[x], solid_held[x], kind_held[x])
         for k in range(6):
             flow[k, x] = values[k]
         total = total + (0.5 * weight_at(start + x, whole_x)) * values[6]
@@ -298,21 +313,43 @@
     ys, out, own = refs[:n], refs[n : n + m], refs[n + m]
     pull = Pull(links, a, ys)
     lane = pull.lane
-    both = []
-    for near, far, moving in ((127, 126, downs[2]), (0, 1, ups[2])):
-        tiles = [jnp.zeros((8, 128), jnp.float32)] * 2
-        for q in range(24):
+    even = lax.axis_index("gz") % 2 == 0
+
+    def source(side, q, x):
+        near, far, moving = ((127, 126, downs[2]), (0, 1, ups[2]))[side]
+        if q < 10:
+            return pull.along_y(moving[q % 5], x), near if q < 5 else far
+        return pull.along_y(flats[2][q - 10], x) if q < 19 else flow[q - 19, x], near
+
+    def gather(side_of, first, last):
+        tile = jnp.zeros((8, 128), jnp.float32)
+        for q in range(first, last):
             for x in range(8):
                 at = (q % 16) * 8 + x
-                if q < 10:
-                    tile, column = pull.along_y(moving[q % 5], x), near if q < 5 else far
-                else:
-                    tile, column = pull.along_y(flats[2][q - 10], x) if q < 19 else flow[q - 19, x], near
-                tiles[q // 16] = jnp.where(lane == at, roll(tile, at - column, 1), tiles[q // 16])
-        both.append(tiles)
+                tile = jnp.where(lane == at, side_of(q, x, at), tile)
+        return tile
+
+    def one_side(side):
+        def value(q, x, at):
+            tile, column = source(side, q, x)
+            return roll(tile, at - column, 1)
+
+        return value
+
+    def facing(first_side):
+        def value(q, x, at):
+            (up, up_at), (down, down_at) = source(0, q, x), source(1, q, x)
+            shift = jnp.where(first_side, at - up_at + 128, at - down_at + 128) & 127
+            return pltpu.roll(jnp.where(first_side, up, down), shift, 1)
+
+        return value
+
     for k in range(2):
-        own[k] = both[k][0]
-        links[2].emit(out, k, both[0][k], both[1][k])
+        own[k] = gather(one_side(k), 0, 5)
+    for c, ref in enumerate(out):
+        first_side = even if c == 0 else jnp.logical_not(even)
+        for k in range(2):
+            ref[k] = gather(facing(first_side), 16 * k, 16 + 8 * k)
 
 
 def pack_x_kernel(links, whole_x, a, flow, own, *refs):
@@ -360,12 +397,25 @@
         links[0].emit(out, k, both[0][k], both[1][k])
 
 
-def step_1_kernel(links, whole_x, a, flow, side, *refs):
+def inner_kernel(links, whole_x, a, flow, *refs):
+    n, m = links[1].count, links[2].count
+    new, sens = refs[n + m + 1 :]
+    pull = Pull(links, a, refs[:n], refs[n : n + m])
+    start = lax.axis_index("gx") * 8
+    for x in range(1, 7):
+        p = [pull.tile(i, x + lattice[i][0]) for i in range(19)]
+        out, s = local_adjoint(p, [flow[k, x] for k in range(5)], weight_at(start + x, whole_x))
+        for i in range(19):
+            new[i, x - 1] = out[i]
+        sens[x - 1] = s * flow[5, x]
+
+
+def step_1_kernel(links, whole_x, a, flow, side, inner, inner_sens, after, *refs):
     n, m, c = links[1].count, links[2].count, links[0].count
     refs = list(refs)
     take = lambda k: [refs.pop(0) for _ in range(k)]
     ys, zs, xs = take(n), take(m), take(c)
-    new, beside_x, beside_z, sens = take(4)
+    ends, beside_x, beside_z, sens = take(4)
     out_y = refs
     pull = Pull(links, a, ys, zs)
     sub, lane = pull.sub, pull.lane
@@ -375,7 +425,7 @@
     below = [links[0].below(xs, k) for k in range(16)]
     first_x, last_x = links[0].ends()
     first_z, last_z = links[2].ends()
-    for x in range(8):
+    for e, x in enumerate((0, 7)):
         p = []
         for i in range(19):
             to = x + lattice[i][0]
@@ -387,8 +437,8 @@
                 p.append(pull.tile(i, to))
         out, s = local_adjoint(p, [flow[k, x] for k in range(5)], weight_at(start + x, whole_x))
         for i in range(19):
-            new[i, x] = out[i]
-        sens[x] = s * flow[5, x]
+            ends[i, e] = out[i]
+        sens[e] = s * flow[5, x]
     for base, near, mine, moving, got, absent in (
         (0, 0, ups[0], downs[0], below, first_x), (5, 7, downs[0], ups[0], above, last_x)
     ):
@@ -398,6 +448,7 @@
         out, _ = local_adjoint(p, got[10:15], 0.0)
         for k, i in enumerate(moving):
             beside_x[base + k] = jnp.where(absent, 0.0, out[i] + got[5 + k])
+
     def at(tile, lane_to, q):
         return roll(tile, lane_to - q, 1)
 
@@ -430,7 +481,11 @@
     for k in range(5):
         beside_z[k] = here * jnp.where(lane < 64, out[z_low[k]], out[z_high[k]])
     for k in range(5):
-        links[1].emit(out_y, k, new[downs[1][k], :, 7, :], new[ups[1][k], :, 0, :])
+        rows = []
+        for i, y in ((downs[1][k], 7), (ups[1][k], 0)):
+            middle = jnp.concatenate([ends[i, 0:1, y, :], inner[i, :, y, :], ends[i, 1:2, y, :]], axis=0)
+            rows.append(middle)
+        links[1].emit(out_y, k, *rows)
     both = []
     for cy, row in ((-1, 7), (1, 0)):
         left = beside_x[downs[0].index(lattice.index((-1, cy, 0)))][row : row + 1, :]
@@ -440,7 +495,7 @@
     links[1].emit(out_y, 5, *both)
 
 
-def step_0_kernel(links, whole_x, a, beside_x, beside_z, flow, sens_in, cost_in, *refs):
+def step_0_kernel(links, whole_x, inner, ends, beside_x, beside_z, flow, inner_sens, end_sens, cost_in, *refs):
     n = links[1].count
     ys = refs[:n]
     new, sens, sums = refs[n:]
@@ -465,14 +520,15 @@
     for x in range(8):
         p = []
         for i in range(19):
-            cx, cy, cz = lattice[i]
+            cx, _, cz = lattice[i]
             to = x + cx
             if to < 0:
                 tile = moved_y(beside_x[downs[0].index(i)], i, 0)
             elif to > 7:
                 tile = moved_y(beside_x[5 + ups[0].index(i)], i, 1)
             else:
-                tile = shift_y(a[i, to], i, to, y_above, y_below, sub)
+                tile = inner[i, to - 1] if 0 < to < 7 else ends[i, to // 7]
+                tile = shift_y(tile, i, to, y_above, y_below, sub)
             if cz:
                 at = 127 if cz == 1 else 0
                 held = (65 if cz == 1 else 1) + to
@@ -481,7 +537,7 @@
         out, s = local_adjoint(p, [flow[k, x] for k in range(5)], weight_at(start + x, whole_x))
         for i in range(19):
             new[i, x] = out[i]
-        s = s * flow[5, x] + sens_in[x]
+        s = s * flow[5, x] + (inner_sens[x - 1] if 0 < x < 7 else end_sens[x // 7])
         squares = squares + s * s
         sens[x] = s
     total = jnp.sum(jnp.sum(cost_in[...], axis=0, keepdims=True))
@@ -489,14 +545,20 @@
     sums[...] = jnp.broadcast_to(both[None], sums.shape)
 
 
-def finish_kernel(cells, got, sens, out, objective, sens_rms):
+def finish_kernel(cells, got, sens, a, out_a, out, objective, sens_rms, held, done):
+    whole = pltpu.make_async_copy(a, out_a, done.at[0])
+    whole.start()
     sums = jnp.sum(got[...], axis=0)
     cost = jnp.sum(sums[:, :1])
     square = jnp.sum(sums[:, 64:65])
     rms = jnp.sqrt(jnp.broadcast_to(square / cells, (1, 128)) + 1e-06)
-    out[...] = sens[...] / jnp.broadcast_to(rms[None], sens.shape)
+    held[...] = sens[...] / jnp.broadcast_to(rms[None], sens.shape)
+    scaled = pltpu.make_async_copy(held, out, done.at[1])
+    scaled.start()
     objective[0, 0] = cost / cells
     sens_rms[0, 0] = jnp.max(rms)
+    scaled.wait()
+    whole.wait()
 
 
 vmem = pl.BlockSpec(memory_space=pltpu.VMEM)
@@ -504,7 +566,7 @@
 hbm = pl.BlockSpec(memory_space=pl.ANY)
 
 
-def call(kernel, outs, *args, name, plain=(), scalar=(), unplaced=(), scratch=(), cost=None):
+def call(kernel, outs, *args, plain=(), scalar=(), unplaced=(), scratch=(), cost=None):
     shapes = tuple(
         jax.ShapeDtypeStruct(s, jnp.float32) if k in plain or k in scalar else pltpu.VMEM(s, jnp.float32)
         for k, s in enumerate(outs)
@@ -514,14 +576,17 @@
         kernel,
         out_shape=shapes,
         in_specs=[hbm if k in unplaced else vmem for k in range(len(args))],
-        out_specs=tuple(smem if k in scalar else vmem for k in range(len(outs))),
+        out_specs=tuple(smem if k in scalar else hbm if k in plain else vmem for k in range(len(outs))),
         scratch_shapes=scratch,
         cost_estimate=cost,
-        name=name,
     )(*args)
 
 
 def body(sizes, a, states, design, solid, kind):
+    return whole_body(sizes, a, states, design, solid, kind)
+
+
+def whole_body(sizes, a, states, design, solid, kind):
     links = [Link(axis, sizes[axis]) for axis in axes]
     devices = sizes["gx"] * sizes["gy"] * sizes["gz"]
     block = design.shape
@@ -529,41 +594,48 @@
     cells = devices * design.size
     whole_x = sizes["gx"] * 8
     tile = (8, 128)
-    held = [pltpu.VMEM(a.shape, jnp.float32), pltpu.SemaphoreType.DMA]
+    held = [pltpu.VMEM(a.shape, jnp.float32), pltpu.VMEM(block, jnp.float32)]
+    held += [pltpu.VMEM(block, jnp.int32)] * 2 + [pltpu.SemaphoreType.DMA((7,))]
     count = pl.CostEstimate(flops=4 * 10**6, bytes_accessed=10**6, transcendentals=0)
 
-    ys = call(partial(pack_y_kernel, links), [(5, *tile)] * links[1].count, a, name="pack_y")
+    ys = call(
+        partial(pack_y_kernel, links), [(5, *tile)] * links[1].count, a, unplaced=(0,),
+        scratch=[pltpu.VMEM((2, 5, *tile), jnp.float32), pltpu.SemaphoreType.DMA((10,))],
+    )
     flow, cost = call(
-        partial(flow_kernel, (1, whole_x)), [(6, *block), tile], states, design, solid, kind, ys[0],
-        name="flow_1", unplaced=(0,), scratch=held, cost=count,
+        partial(flow_kernel, 1, whole_x), [(6, *block), tile], states, design, solid, kind, ys[0],
+        unplaced=(0, 1, 2, 3), scratch=held, cost=count,
     )
     ys = links[1].swap(ys)
-    *zs, own = call(
-        partial(pack_z_kernel, links), [(2, *tile)] * (links[2].count + 1), a, flow, *ys, name="pack_z"
-    )
+    *zs, own = call(partial(pack_z_kernel, links), [(2, *tile)] * (links[2].count + 1), a, flow, *ys)
     zs = links[2].swap(zs)
     *xs, side = call(
         partial(pack_x_kernel, links, whole_x), [(16, *tile)] * links[0].count + [(24, *tile)],
-        a, flow, own, *ys, *zs, name="pack_x",
+        a, flow, own, *ys, *zs,
     )
     flow_0, cost = call(
-        partial(flow_kernel, (0, whole_x)), [(6, *block), tile], states, design, solid, kind, xs[-1], cost,
-        name="flow_0", unplaced=(0,), scratch=held, cost=count,
+        partial(flow_kernel, 0, whole_x), [(6, *block), tile], states, design, solid, kind, xs[-1], cost,
+        unplaced=(0, 1, 2, 3), scratch=held, cost=count,
+    )
+    inner, inner_sens = call(
+        partial(inner_kernel, links, whole_x), [(19, 6, *tile), (6, *tile)], a, flow, *ys, *zs, xs[-1],
+        cost=count,
     )
     xs = links[0].swap(xs)
-    a, beside_x, beside_z, sens, *ys = call(
+    ends, beside_x, beside_z, end_sens, *ys = call(
         partial(step_1_kernel, links, whole_x),
-        [a.shape, (10, *tile), (5, *tile), block] + [(6, *tile)] * links[1].count,
-        a, flow, side, *ys, *zs, *xs, name="step_1",
+        [(19, 2, *tile), (10, *tile), (5, *tile), (2, *tile)] + [(6, *tile)] * links[1].count,
+        a, flow, side, inner, inner_sens, cost, *ys, *zs, *xs,
     )
     ys = links[1].swap(ys)
     a, sens, sums = call(
         partial(step_0_kernel, links, whole_x), [a.shape, block, (devices, 1, 128)],
-        a, beside_x, beside_z, flow_0, sens, cost, *ys, name="step_0", plain=(0,),
+        inner, ends, beside_x, beside_z, flow_0, inner_sens, end_sens, cost, *ys,
     )
     got = lax.all_to_all(sums, axes, 0, 0)
-    sens, objective, sens_rms = call(
-        partial(finish_kernel, cells), [block, (1, 1), (1, 1)], got, sens, name="finish", plain=(0,), scalar=(1, 2)
+    a, sens, objective, sens_rms = call(
+        partial(finish_kernel, cells), [a.shape, block, (1, 1), (1, 1)], got, sens, a,
+        plain=(0, 1), scalar=(2, 3), scratch=[pltpu.VMEM(block, jnp.float32), pltpu.SemaphoreType.DMA((2,))],
     )
     return a, sens, objective.reshape(()), sens_rms.reshape(())
 

time: 36.7 us -> 33.4 us (0.910)
  local copies, waits for them, and re-layouts: 3.36 us -> 0.01 us
  Pallas kernels: 6.11 us -> 7.13 us
  waiting for transfers between devices: 3.22 us -> 2.82 us
    unnamed x16 -> x2, local copies, waits for them, and re-layouts: 3.36 us -> 0.01 us
    pallas_call x8 -> x9, Pallas kernels: 6.11 us -> 7.13 us  [call(): pl.pallas_call(kernel, out_shape=shapes, in_specs=[hbm if k in unplaced e...]
    ppermute x5, waiting for transfers between devices: 3.22 us -> 2.82 us  [swap(): got.append(lax.ppermute(m, self.axis, swap_pairs(self.size, k)))]
  transfers between devices with their start and end apart: 5 -> 5, of which waited for: 2 -> 2; matrix products, arithmetic and copies ran while one was open for 0% -> 0% of each run, Pallas kernels for 6% -> 9%
where the time goes in v4:
time: 33.4 us; the launch traced here: 33.2 us
  blocking collectives  16.5 us (49%)
  Pallas kernels  7.13 us (21%)
  starting transfers between devices  5.95 us (18%)
  waiting for transfers between devices  2.82 us (8%)
  between operations  0.75 us (2%)
    all_to_all x1, blocking collectives, whole_body(): got = lax.all_to_all(sums, axes, 0, 0)  16.5 us
    pallas_call x9, Pallas kernels, call(): pl.pallas_call(kernel, out_shape=shapes, in_specs=[hbm if k in unplaced e...  7.13 us
    ppermute x5, starting transfers between devices, swap(): got.append(lax.ppermute(m, self.axis, swap_pairs(self.size, k)))  5.95 us
    ppermute x5, waiting for transfers between devices, swap(): got.append(lax.ppermute(m, self.axis, swap_pairs(self.size, k)))  2.82 us
  transfers between devices with their start and end apart: 5, of which 2 were waited for; matrix products, arithmetic and copies ran while one was open for 0% of the time, Pallas kernels for 9%

profile of v4, /device:TPU:0, one launch (start us, length us, event | category | flops | bytes accessed | tf_op | source)
XLA Modules:
  0.0 33.2 jit_solution(3490984879123452242)
XLA Ops:
  0.6 0.0 copy-start
  0.6 1.0 %shard_map.84.after = f32[5,8,128]{2,1,0:T(8,128)S(1)} custom-call(f32[19,8,8,128]{3,2,1,0:T(8,128)} %a.9), custom_call_target="tpu_custom_call" | custom-call | tf_op jit(solution)/shard_map/pallas_call | solution.py:575
  1.6 0.6 %collective-permute-start = (f32[5,8,128]{2,1,0:T(8,128)S(1)}, f32[5,8,128]{2,1,0:T(8,128)S(1)}, u32[]{:S(2)}, u32[]{:S(2)}) collective-permute-start(f32[5,8,128]{2,1,0:T(8,128)S(1)} %shard_map.84.after), channel_id=1, source_target_pairs={{0,2},{2,0},{1,3},{3,1},{4,6},{6,4},{5,7},{7,5},{8,10},{10,8},{9,1... | collective-permute-start | bytes 61448 | tf_op jit(solution)/shard_map/ppermute | solution.py:187
  2.2 1.3 %shard_map.85 = (f32[6,8,8,128]{3,2,1,0:T(8,128)S(1)}, f32[8,128]{1,0:T(8,128)S(1)}) custom-call(f32[2,19,8,8,128]{4,3,2,1,0:T(8,128)} %states.3, f32[8,8,128]{2,1,0:T(8,128)} %g.3, s32[8,8,128]{2,1,0:T(8,128)} %solid.3, s32[8,8,128]{2,1,0:T(8,128)} %kind.3, f32[5,8,128]{2,1,0:T(8,128)S(1)} %shard_map.84.after), custom_call_target="tpu_custom_call" | custom-call | flops 4000000 | bytes 1000000 | tf_op jit(solution)/shard_map/pallas_call | solution.py:575
  3.5 0.0 collective-permute-done.refs_0_
  3.5 0.0 copy-done
  3.5 0.4 %shard_map.86 = (f32[2,8,128]{2,1,0:T(8,128)S(1)}, f32[2,8,128]{2,1,0:T(8,128)S(1)}) custom-call(f32[19,8,8,128]{3,2,1,0:T(8,128)S(1)} %copy-done, f32[6,8,8,128]{3,2,1,0:T(8,128)S(1)} %get-tuple-element.27.flow, f32[5,8,128]{2,1,0:T(8,128)S(1)} %collective-permute-done.refs_0_), custom_call_target="tpu_custom_call" | custom-call | tf_op jit(solution)/shard_map/pallas_call | solution.py:575
  3.9 2.6 %collective-permute-start.1 = (f32[2,8,128]{2,1,0:T(8,128)S(1)}, f32[2,8,128]{2,1,0:T(8,128)S(1)}, u32[]{:S(2)}, u32[]{:S(2)}) collective-permute-start(f32[2,8,128]{2,1,0:T(8,128)S(1)} %get-tuple-element.28), channel_id=1, source_target_pairs={{0,1},{1,0},{2,3},{3,2},{4,5},{5,4},{6,7},{7,6},{8,9},{9,8},{10,11... | collective-permute-start | bytes 24584 | tf_op jit(solution)/shard_map/ppermute | solution.py:187
  6.4 1.6 %collective-permute-done.1.refs_1_ = f32[2,8,128]{2,1,0:T(8,128)S(1)} collective-permute-done((f32[2,8,128]{2,1,0:T(8,128)S(1)}, f32[2,8,128]{2,1,0:T(8,128)S(1)}, u32[]{:S(2)}, u32[]{:S(2)}) %collective-permute-start.1) | collective-permute-done | bytes 8224 | tf_op jit(solution)/shard_map/ppermute | solution.py:187
  8.0 0.2 shard_map.87
  8.3 2.1 %collective-permute-start.2 = (f32[16,8,128]{2,1,0:T(8,128)S(1)}, f32[16,8,128]{2,1,0:T(8,128)S(1)}, u32[]{:S(2)}, u32[]{:S(2)}) collective-permute-start(f32[16,8,128]{2,1,0:T(8,128)S(1)} %get-tuple-element.36), channel_id=1, source_target_pairs={{0,4},{4,0},{8,12},{12,8},{16,20},{20,16},{24,28},{28,24},{1,5},{5... | collective-permute-start | bytes 196616 | tf_op jit(solution)/shard_map/ppermute | solution.py:187
  10.4 0.7 %collective-permute-start.3 = (f32[16,8,128]{2,1,0:T(8,128)S(1)}, f32[16,8,128]{2,1,0:T(8,128)S(1)}, u32[]{:S(2)}, u32[]{:S(2)}) collective-permute-start(f32[16,8,128]{2,1,0:T(8,128)S(1)} %get-tuple-element.30.refs_2_.after), channel_id=1, source_target_pairs={{0,0},{4,8},{8,4},{12,16},{16,12},{20,24},{24,20},{28,28},{1,1},{5... | collective-permute-start | bytes 196616 | tf_op jit(solution)/shard_map/ppermute | solution.py:187
  11.1 1.3 %shard_map.89 = (f32[6,8,8,128]{3,2,1,0:T(8,128)S(1)}, f32[8,128]{1,0:T(8,128)S(1)}) custom-call(f32[2,19,8,8,128]{4,3,2,1,0:T(8,128)} %states.3, f32[8,8,128]{2,1,0:T(8,128)} %g.3, s32[8,8,128]{2,1,0:T(8,128)} %solid.3, s32[8,8,128]{2,1,0:T(8,128)} %kind.3, f32[16,8,128]{2,1,0:T(8,128)S(1)} %get-tuple-element.30.refs_2_.after, ...), custom_call_target="tpu_custom_call" | custom-call | flops 4000000 | bytes 1000000 | tf_op jit(solution)/shard_map/pallas_call | solution.py:575
  12.4 0.5 %shard_map.88 = (f32[19,6,8,128]{3,2,1,0:T(8,128)S(1)}, f32[6,8,128]{2,1,0:T(8,128)S(1)}) custom-call(f32[19,8,8,128]{3,2,1,0:T(8,128)S(1)} %copy-done, f32[6,8,8,128]{3,2,1,0:T(8,128)S(1)} %get-tuple-element.27.flow, f32[5,8,128]{2,1,0:T(8,128)S(1)} %collective-permute-done.refs_0_, f32[2,8,128]{2,1,0:T(8,128)S(1)} %collective-permute-done.1.refs_1_, ...), custom_call_target="tpu_custom_call" | custom-call | flops 4000000 | bytes 1000000 | tf_op jit(solution)/shard_map/pallas_call | solution.py:575
  12.8 0.0 collective-permute-done.2.refs_2_
  12.8 0.0 collective-permute-done.3.refs_3_
  12.9 0.4 %shard_map.90 = (f32[19,2,8,128]{3,2,1,0:T(8,128)S(1)}, f32[10,8,128]{2,1,0:T(8,128)S(1)}, f32[5,8,128]{2,1,0:T(8,128)S(1)}, f32[2,8,128]{2,1,0:T(8,128)S(1)}, f32[6,8,128]{2,1,0:T(8,128)S(1)}) custom-call(f32[19,8,8,128]{3,2,1,0:T(8,128)S(1)} %copy-done, f32[6,8,8,128]{3,2,1,0:T(8,128)S(1)} %get-tuple-element.27.flow, ...), custom_call_target="tpu_custom_call" | custom-call | tf_op jit(solution)/shard_map/pallas_call | solution.py:575
  13.3 0.1 collective-permute-start.4
  13.3 1.2 %collective-permute-done.4.refs_0_ = f32[6,8,128]{2,1,0:T(8,128)S(1)} collective-permute-done((f32[6,8,128]{2,1,0:T(8,128)S(1)}, f32[6,8,128]{2,1,0:T(8,128)S(1)}, u32[]{:S(2)}, u32[]{:S(2)}) %collective-permute-start.4) | collective-permute-done | bytes 24608 | tf_op jit(solution)/shard_map/ppermute | solution.py:187
  14.5 0.7 %shard_map.91 = (f32[19,8,8,128]{3,2,1,0:T(8,128)S(1)}, f32[8,8,128]{2,1,0:T(8,128)S(1)}, f32[32,1,128]{2,1,0:T(1,128)S(1)}) custom-call(f32[19,6,8,128]{3,2,1,0:T(8,128)S(1)} %get-tuple-element.31.inner, f32[19,2,8,128]{3,2,1,0:T(8,128)S(1)} %get-tuple-element.37.ends, f32[10,8,128]{2,1,0:T(8,128)S(1)} %get-tuple-element.38.beside_x, ...), custom_call_target="tpu_custom_call" | custom-call | tf_op jit(solution)/shard_map/pallas_call | solution.py:575
  15.3 16.5 %all_to_all.5.got = f32[32,1,128]{2,1,0:T(1,128)S(1)} all-to-all(f32[32,1,128]{2,1,0:T(1,128)S(1)} %get-tuple-element.43), channel_id=1, replica_groups=mesh['gx'=8,'gy'=2,'gz'=2] {'gx','gy','gz'}, dimensions={0} | all-to-all | bytes 32768 | tf_op jit(solution)/shard_map/all_to_all | solution.py:635
  31.8 1.4 %shard_map.92 = (f32[19,8,8,128]{3,2,1,0:T(8,128)}, f32[8,8,128]{2,1,0:T(8,128)}, f32[1,1]{1,0:T(1,128)}, f32[1,1]{1,0:T(1,128)}) custom-call(f32[32,1,128]{2,1,0:T(1,128)S(1)} %all_to_all.5.got, f32[8,8,128]{2,1,0:T(8,128)S(1)} %get-tuple-element.44.sens, f32[19,8,8,128]{3,2,1,0:T(8,128)S(1)} %get-tuple-element.45.a), custom_call_target="tpu_custom_call" | custom-call | tf_op jit(solution)/shard_map/pallas_call | solution.py:575
Async XLA Ops:
  0.6 2.9 %copy-start = (f32[19,8,8,128]{3,2,1,0:T(8,128)S(1)}, f32[19,8,8,128]{3,2,1,0:T(8,128)}, u32[]{:S(2)}) copy-start(f32[19,8,8,128]{3,2,1,0:T(8,128)} %a.9) | copy-start | bytes 1867780
  1.6 1.9 %collective-permute-start = (f32[5,8,128]{2,1,0:T(8,128)S(1)}, f32[5,8,128]{2,1,0:T(8,128)S(1)}, u32[]{:S(2)}, u32[]{:S(2)}) collective-permute-start(f32[5,8,128]{2,1,0:T(8,128)S(1)} %shard_map.84.after), channel_id=1, source_target_pairs={{0,2},{2,0},{1,3},{3,1},{4,6},{6,4},{5,7},{7,5},{8,10},{10,8},{9,1... | collective-permute-start | bytes 61448 | tf_op jit(solution)/shard_map/ppermute | solution.py:187
  3.9 4.2 %collective-permute-start.1 = (f32[2,8,128]{2,1,0:T(8,128)S(1)}, f32[2,8,128]{2,1,0:T(8,128)S(1)}, u32[]{:S(2)}, u32[]{:S(2)}) collective-permute-start(f32[2,8,128]{2,1,0:T(8,128)S(1)} %get-tuple-element.28), channel_id=1, source_target_pairs={{0,1},{1,0},{2,3},{3,2},{4,5},{5,4},{6,7},{7,6},{8,9},{9,8},{10,11... | collective-permute-start | bytes 24584 | tf_op jit(solution)/shard_map/ppermute | solution.py:187
  8.3 4.6 %collective-permute-start.2 = (f32[16,8,128]{2,1,0:T(8,128)S(1)}, f32[16,8,128]{2,1,0:T(8,128)S(1)}, u32[]{:S(2)}, u32[]{:S(2)}) collective-permute-start(f32[16,8,128]{2,1,0:T(8,128)S(1)} %get-tuple-element.36), channel_id=1, source_target_pairs={{0,4},{4,0},{8,12},{12,8},{16,20},{20,16},{24,28},{28,24},{1,5},{5... | collective-permute-start | bytes 196616 | tf_op jit(solution)/shard_map/ppermute | solution.py:187
  10.4 2.5 %collective-permute-start.3 = (f32[16,8,128]{2,1,0:T(8,128)S(1)}, f32[16,8,128]{2,1,0:T(8,128)S(1)}, u32[]{:S(2)}, u32[]{:S(2)}) collective-permute-start(f32[16,8,128]{2,1,0:T(8,128)S(1)} %get-tuple-element.30.refs_2_.after), channel_id=1, source_target_pairs={{0,0},{4,8},{8,4},{12,16},{16,12},{20,24},{24,20},{28,28},{1,1},{5... | collective-permute-start | bytes 196616 | tf_op jit(solution)/shard_map/ppermute | solution.py:187
  13.3 1.3 %collective-permute-start.4 = (f32[6,8,128]{2,1,0:T(8,128)S(1)}, f32[6,8,128]{2,1,0:T(8,128)S(1)}, u32[]{:S(2)}, u32[]{:S(2)}) collective-permute-start(f32[6,8,128]{2,1,0:T(8,128)S(1)} %get-tuple-element.42), channel_id=1, source_target_pairs={{0,2},{2,0},{1,3},{3,1},{4,6},{6,4},{5,7},{7,5},{8,10},{10,8},{9,1... | collective-permute-start | bytes 73736 | tf_op jit(solution)/shard_map/ppermute | solution.py:187
